TPU v7x, 32 devices: a whole 2x2x4 slice. The times are simulated.
32 devices in a mesh: chain: 4 (over x, core), depth: 8 (over z, y).
Axes of the slice: x: 2, y: 2, z: 4, core: 2. Of those that a mesh axis runs over, the one named last changes fastest.
Arguments:
- model_field: float32 [256, 2048], P(('chain', 'depth')), parts along dimension 0, may hold values from -4 to 4
- column_rate: float32 [8192], P('chain'), parts along dimension 0, may hold values from 0.2 to 20
- wavelets: float32 [64, 2048], P('chain'), parts along dimension 0, may hold values from -6 to 6
- source_depth: int32 [64], P('chain'), parts along dimension 0, may hold values from 0 to 63
- observed: float32 [256, 16, 2048], P(('chain', 'depth')), parts along dimension 0, may hold values from -3 to 3
- basis: bfloat16 [1024, 64, 2048], P('chain', 'depth'), parts along dimension 0, may hold values from -0.0625 to 0.0625
- curvature: float32 [1024], P('chain'), parts along dimension 0, may hold values from 0.5 to 50
- noise_draw: float32 [256, 2048], P(('chain', 'depth')), parts along dimension 0, may hold values from -6 to 6
Outputs:
- proposal: float32 [256, 2048], P(('chain', 'depth')), parts along dimension 0
- log_gain: float32 [4], P('chain'), parts along dimension 0
There are 4 independent parts, one for each index of `chain`. A program takes and returns all parts, laid end to end along the dimension named above; each array names one. Nothing has to cross between parts.
All inputs are finite; a program needn't handle non-finite values.
Results may differ from a plain program's by a relative error of at most 0.0003.
The roundings to bfloat16 on the way count: a program that leaves them out, or rounds other values in their place, can miss the bound.
Values sent between devices are 32-bit elements; how exact they have to be, the bound alone decides.
No kernel may reach another device: no remote copies, remote signals or barrier semaphores. Data moves between devices by JAX's collectives and lax.ppermute only.
A program may use at most 64 MiB of HBM per device.

v0:
```python
import jax
import jax.numpy as jnp
from jax import lax
from jax.sharding import PartitionSpec as P


def from_gathered(log_block, outgoing, upward):
    logs, ends = (
        lax.all_gather(log_block[None], "depth", axis=0, tiled=True),
        lax.all_gather(outgoing[None], "depth", axis=0, tiled=True),
    )
    index = lax.axis_index("depth")
    prefix = jnp.cumsum(logs, axis=0)
    mine = lax.dynamic_index_in_dim(prefix, index, 0, keepdims=False)
    order = jnp.arange(logs.shape[0], dtype=jnp.int32)[:, None]
    if upward:
        exponent = prefix - logs - mine[None, :]
        keep = order > index
    else:
        exponent = mine[None, :] - log_block[None, :] - prefix
        keep = order < index
    weights = jnp.where(keep, jnp.exp(jnp.minimum(exponent, 0.0)), 0.0)
    return jnp.sum(weights[:, None, :] * ends, axis=0)


def enter_down(log_block, outgoing):
    return from_gathered(log_block, outgoing, False)


def enter_up(log_block, outgoing):
    return from_gathered(log_block, outgoing, True)


def march_down(model, column_rate, wavelets, source_depth, depth_count):
    coef = (column_rate / depth_count)[None, :] * jnp.exp(0.5 * model)
    decay = jnp.exp(-coef)
    running = jnp.cumsum(coef, axis=0)
    first = lax.axis_index("depth") * model.shape[0]
    layers = first + jnp.arange(model.shape[0], dtype=jnp.int32)

    def advance(state, inputs):
        factor, layer = inputs
        inject = jnp.where((source_depth == layer)[:, None], wavelets, jnp.zeros_like(wavelets))
        state = factor[None, :] * state + inject
        return (state, state)

    start = jnp.zeros(wavelets.shape, jnp.float32)
    last, fields = lax.scan(advance, start, (decay, layers))
    carry = enter_down(-running[-1], last)
    fields = fields + jnp.exp(-running)[:, None, :] * carry[None]
    return (coef, decay, running, carry, fields)


def local(model_field, column_rate, wavelets, source_depth, observed, basis, curvature, noise_draw):
    depth_count = model_field.shape[0] * lax.axis_size("depth")
    sources = wavelets.shape[0]
    coef, decay, running, carry, fields = march_down(
        model_field, column_rate, wavelets, source_depth, depth_count
    )
    resid = fields - observed
    energy_now = jnp.sum(resid * resid) / sources + 0.5 * jnp.sum(model_field * model_field)

    def retreat(state, inputs):
        factor, residual_layer = inputs
        adjoint = residual_layer + state
        return (factor[None, :] * adjoint, adjoint)

    upper, adjoints = lax.scan(
        retreat, jnp.zeros(resid.shape[1:], jnp.float32), (decay, resid), reverse=True
    )
    below = enter_up(-running[-1], upper)
    adjoints = adjoints + jnp.exp(running - running[-1:])[:, None, :] * below[None]
    previous = jnp.concatenate([carry[None], fields[:-1]], axis=0)
    gradient = model_field - coef * decay / sources * jnp.sum(adjoints * previous, axis=1)
    flat_basis = basis.reshape(basis.shape[0], -1)
    stacked = jnp.stack([gradient.reshape(-1), noise_draw.reshape(-1)]).astype(jnp.bfloat16)
    local_proj = lax.dot_general(
        stacked, flat_basis, (((1,), (1,)), ((), ())), preferred_element_type=jnp.float32
    )
    projected, energy_total = lax.psum((local_proj, energy_now), "depth")
    damping = curvature / (1.0 + curvature)
    shrink = 1.0 - 1.0 / jnp.sqrt(1.0 + curvature)
    mixed = (damping * projected[0] - shrink * projected[1]).astype(jnp.bfloat16)
    correction = jnp.dot(mixed, flat_basis, preferred_element_type=jnp.float32).reshape(
        model_field.shape
    )
    proposal = model_field - gradient + noise_draw + correction
    fields_next = march_down(proposal, column_rate, wavelets, source_depth, depth_count)[4]
    resid_next = fields_next - observed
    energy_next = jnp.sum(resid_next * resid_next) / sources + 0.5 * jnp.sum(proposal * proposal)
    after = lax.psum(energy_next, "depth")
    cells = depth_count * model_field.shape[1]
    log_gain = jnp.reshape((energy_total - after) / cells, (1,))
    return (proposal, log_gain)


def solution(mesh):
    in_specs = (
        P(("chain", "depth"), None),
        P("chain"),
        P("chain", None),
        P("chain"),
        P(("chain", "depth"), None, None),
        P("chain", "depth", None),
        P("chain"),
        P(("chain", "depth"), None),
    )
    out_specs = (P(("chain", "depth"), None), P("chain"))
    return jax.shard_map(local, mesh=mesh, in_specs=in_specs, out_specs=out_specs, check_vma=False)
```

profile of v0, /device:TPU:0, one launch (start us, length us, event | category | flops | bytes accessed | tf_op | source)
XLA Modules:
  0.0 242.2 jit_solution(17946942352348983810)
XLA Ops:
  8.9 23.4 %while.43 = (s32[]{:T(128)}, f32[16,2048]{1,0:T(8,128)S(1)}, f32[8,16,2048]{2,1,0:T(8,128)S(1)}, f32[8,2048]{1,0:T(8,128)S(1)}, s32[8]{0:T(128)S(1)}, /*index=5*...) while((s32[]{:T(128)}, f32[16,2048]{1,0:T(8,128)S(1)}, f32[8,16,2048]{2,1,0:T(8,128)S(1)}, ...), condition=%wide.region_1.2_spmd.clone, body=%wide.region_0.0_spmd.clone.sunk | while | flops 131091 | bytes 549583 | solution.py:48
  9.5 1.3 broadcast_compare_fusion.4
  10.8 1.0 bitcast_dynamic-update-slice_fusion.6
  12.4 1.3 broadcast_compare_fusion.4
  13.8 1.0 bitcast_dynamic-update-slice_fusion.6
  15.4 1.3 broadcast_compare_fusion.4
  16.7 1.0 bitcast_dynamic-update-slice_fusion.6
  18.3 1.3 broadcast_compare_fusion.4
  19.6 1.0 bitcast_dynamic-update-slice_fusion.6
  21.2 1.3 broadcast_compare_fusion.4
  22.5 1.0 bitcast_dynamic-update-slice_fusion.6
  24.1 1.3 broadcast_compare_fusion.4
  25.5 1.0 bitcast_dynamic-update-slice_fusion.6
  27.1 1.3 broadcast_compare_fusion.4
  28.4 1.0 bitcast_dynamic-update-slice_fusion.6
  30.0 1.3 broadcast_compare_fusion.4
  31.3 1.0 bitcast_dynamic-update-slice_fusion.6
  33.2 32.5 %all-gather.3 = f32[8,1,2048]{2,1,0:T(1,128)S(1)} all-gather(f32[1,1,2048]{2,1,0:T(1,128)S(1)} %get-tuple-element.314), channel_id=1, replica_groups=mesh['chain'=4,'depth'=8] {'depth'}, dimensions={0}, use_global_device_ids=true | all-gather | bytes 73728 | tf_op jit(solution)/shard_map/all_gather | solution.py:9
  67.2 9.2 %all-gather.9.cloned.1.call-done = f32[128,2048]{1,0:T(8,128)} async-done(((f32[16,2048]{1,0:T(8,128)}), f32[128,2048]{1,0:T(8,128)}) %all-gather.9.cloned.1.call-update) | async-done | bytes 1048592 | tf_op jit(solution)/shard_map/all_gather | solution.py:10
  76.4 1.3 multiply_reduce_fusion.4
  77.7 2.2 multiply_reduce_fusion.2
  81.8 16.2 %copy.17 = bf16[32,8,8,2048]{3,1,2,0:T(8,128)(2,1)} copy(bf16[32,8,8,2048]{3,2,1,0:T(8,128)(2,1)} %bitcast.85) | data formatting | bytes 16777216
  98.2 22.7 %all-gather.11.cloned.1.call-done = f32[128,2048]{1,0:T(8,128)} async-done(((f32[16,2048]{1,0:T(8,128)}), f32[128,2048]{1,0:T(8,128)}) %all-gather.11.cloned.1.call-update) | async-done | bytes 1048592 | tf_op jit(solution)/shard_map/all_gather | solution.py:10
  120.9 1.3 multiply_reduce_fusion.3
  123.3 5.7 %fusion.6 = f32[2,256]{1,0:T(2,128)S(1)} fusion(bf16[256,16384]{1,0:T(8,128)(2,1)} %bitcast.84, bf16[1,16384]{1,0:T(2,128)(2,1)S(1)} %bitcast.94, bf16[1,16384]{1,0:T(2,128)(2,1)S(1)} %bitcast.95), kind=kOutput, calls=%fused_computation.25 | convolution fusion | flops 16908288 | bytes 8456192 | tf_op jit(solution)/shard_map/dot_general | solution.py:77
  129.0 19.5 %psum.21 = f32[2,256]{1,0:T(2,128)S(1)} all-reduce(f32[2,256]{1,0:T(2,128)S(1)} %fusion.6), channel_id=1, replica_groups=mesh['chain'=4,'depth'=8] {'depth'}, use_global_device_ids=true, to_apply=%region_9.10 | all-reduce | flops 512 | bytes 4096 | tf_op jit(solution)/shard_map/psum | solution.py:80
  148.5 12.3 %fusion.2 = f32[1,8,2048]{2,0,1:T(1,128)S(1)} fusion(bf16[256,1,1]{0,1,2:T(2,128)(2,1)S(1)} %reshape.124, bf16[32,8,8,2048]{3,2,1,0:T(8,128)(2,1)} %bitcast.86), kind=kOutput, calls=%fused_computation.14 | convolution fusion | flops 8388608 | bytes 8454656 | tf_op jit(solution)/shard_map/dot_general | solution.py:84
  161.6 10.5 %while.45 = (s32[]{:T(128)}, f32[16,2048]{1,0:T(8,128)S(1)}, f32[8,16,2048]{2,1,0:T(8,128)S(1)}, f32[8,2048]{1,0:T(8,128)S(1)}, s32[8]{0:T(128)S(1)}, /*index=5*...) while((s32[]{:T(128)}, f32[16,2048]{1,0:T(8,128)S(1)}, ...), condition=%wide.region_14.15_spmd.clone, body=%wide.region_13.14_spmd.clone.sunk | while | flops 131091 | bytes 549583 | solution.py:48
  173.5 30.8 %all-gather.4 = f32[8,1,2048]{2,1,0:T(1,128)S(1)} all-gather(f32[1,1,2048]{2,1,0:T(1,128)S(1)} %fusion.15), channel_id=1, replica_groups=mesh['chain'=4,'depth'=8] {'depth'}, dimensions={0}, use_global_device_ids=true | all-gather | bytes 73728 | tf_op jit(solution)/shard_map/all_gather | solution.py:9
  205.8 4.8 %all-gather.13.cloned.1.call-done = f32[128,2048]{1,0:T(8,128)} async-done(((f32[16,2048]{1,0:T(8,128)}), f32[128,2048]{1,0:T(8,128)}) %all-gather.13.cloned.1.call-update) | async-done | bytes 1048592 | tf_op jit(solution)/shard_map/all_gather | solution.py:10
  210.5 1.3 multiply_reduce_fusion.1
  213.4 19.8 %all-reduce = (f32[]{:T(128)}, f32[]{:T(128)}) all-reduce(f32[]{:T(128)S(6)} %add.90, f32[]{:T(128)S(6)} %add.92), channel_id=1, replica_groups=mesh['chain'=4,'depth'=8] {'depth'}, use_global_device_ids=true, to_apply=%region_12.13 | all-reduce | flops 2 | bytes 16 | tf_op jit(solution)/shard_map/psum | solution.py:80
  (145 shorter events, 25.2 us)
Async XLA Ops:
  7.2 69.2 %all-gather.9.cloned.1.call-start = ((), (), s32[]{:S(2)}) async-start(), calls=%async_computation | async-start | bytes 1179648 | tf_op jit(solution)/shard_map/all_gather | solution.py:10
  32.3 0.6 copy-start.3
  32.3 0.7 copy-start.13
  33.0 87.9 %all-gather.11.cloned.1.call-start = ((), (), s32[]{:S(2)}) async-start(), calls=%async_computation.1 | async-start | bytes 1179648 | tf_op jit(solution)/shard_map/all_gather | solution.py:10
  81.0 0.7 copy-start
  81.7 128.9 %all-gather.13.cloned.1.call-start = ((), (), s32[]{:S(2)}) async-start(), calls=%async_computation.2 | async-start | bytes 1179648 | tf_op jit(solution)/shard_map/all_gather | solution.py:10
  81.7 16.3 %copy-start.9 = (f32[8,2048]{1,0:T(8,128)S(1)}, f32[8,2048]{1,0:T(8,128)}, u32[]{:S(2)}) copy-start(f32[8,2048]{1,0:T(8,128)} %param.21) | copy-start | bytes 196612
  81.8 39.2 %copy-start.7 = (f32[8,2048]{1,0:T(8,128)S(1)}, f32[8,2048]{1,0:T(8,128)}, u32[]{:S(2)}) copy-start(f32[8,2048]{1,0:T(8,128)} %get-tuple-element.315) | copy-start | bytes 196612
  81.8 40.5 %copy-start.6 = (f32[8,2048]{1,0:T(8,128)S(1)}, f32[8,2048]{1,0:T(8,128)}, u32[]{:S(2)}) copy-start(f32[8,2048]{1,0:T(8,128)} %get-tuple-element.311) | copy-start | bytes 196612
  81.8 40.8 %copy-start.5 = (f32[8,2048]{1,0:T(8,128)S(1)}, f32[8,2048]{1,0:T(8,128)}, u32[]{:S(2)}) copy-start(f32[8,2048]{1,0:T(8,128)} %param.14) | copy-start | bytes 196612
  98.0 50.4 %copy-start.11 = (f32[256]{0:T(256)S(1)}, f32[256]{0:T(256)}, u32[]{:S(2)}) copy-start(f32[256]{0:T(256)} %param.20) | copy-start | bytes 3076
  123.3 37.5 %copy-start.10 = (f32[8,2048]{1,0:T(8,128)S(1)}, f32[8,2048]{1,0:T(8,128)}, u32[]{:S(2)}) copy-start(f32[8,2048]{1,0:T(8,128)} %param.21) | copy-start | bytes 196612
  128.9 32.6 %copy-start.1 = (f32[16,2048]{1,0:T(8,128)S(1)}, f32[16,2048]{1,0:T(8,128)}, u32[]{:S(2)}) copy-start(f32[16,2048]{1,0:T(8,128)} %get-tuple-element.529) | copy-start | bytes 393220
  128.9 32.6 %copy-start.12 = (s32[16]{0:T(128)S(1)}, s32[16]{0:T(128)}, u32[]{:S(2)}) copy-start(s32[16]{0:T(128)} %get-tuple-element.538) | copy-start | bytes 196
  128.9 32.6 %copy-start.14 = (s32[8]{0:T(128)S(1)}, s32[8]{0:T(128)}, u32[]{:S(2)}) copy-start(s32[8]{0:T(128)} %copy-done.13) | copy-start | bytes 100
  148.5 63.4 %copy-start.4 = (f32[8,16,2048]{2,1,0:T(8,128)S(1)}, f32[8,16,2048]{2,1,0:T(8,128)}, u32[]{:S(2)}) copy-start(f32[8,16,2048]{2,1,0:T(8,128)} %param.18) | copy-start | bytes 3145732
  161.4 73.2 %copy-start.8 = (f32[8,2048]{1,0:T(8,128)}, f32[8,2048]{1,0:T(8,128)S(1)}, u32[]{:S(2)}) copy-start(f32[8,2048]{1,0:T(8,128)S(1)} %get-tuple-element.299) | copy-start | bytes 196612
  172.1 0.6 copy-start.2
Sparse Core Ops, SparseCore 0:
  33.1 43.2 all-gather.8
  81.8 39.0 all-gather.10
  172.9 37.6 all-gather.12
where the time goes:
time: 243 us; the launch traced here: 242 us
  blocking collectives  103 us (42%)
  waiting for transfers between devices  36.8 us (15%)
  other arithmetic  36.4 us (15%)
  local copies, waits for them, and re-layouts  28.4 us (12%)
  between operations  19.1 us (8%)
  matrix products  17.9 us (7%)
    all_gather x2, blocking collectives, from_gathered(): lax.all_gather(log_block[None], 'depth', axis=0, tiled=True)  63.4 us
    psum x2, blocking collectives, local(): projected, energy_total = lax.psum((local_proj, energy_now), 'depth')  39.3 us
    all_gather x3, waiting for transfers between devices, from_gathered(): lax.all_gather(outgoing[None], 'depth', axis=0, tiled=True)  36.8 us
    unnamed x35, local copies, waits for them, and re-layouts  18.4 us
    eq x16, other arithmetic, advance(): source_depth == layer  15.1 us
    dot_general x1, matrix products, local(): jnp.dot(mixed, flat_basis, preferred_element_type=jnp.float32)  12.3 us
    dynamic_slice x40, local copies, waits for them, and re-layouts, march_down(): last, fields = lax.scan(advance, start, (decay, layers))  9.73 us
    dynamic_update_slice x24, other arithmetic, march_down(): last, fields = lax.scan(advance, start, (decay, layers))  8.88 us
  transfers between devices with their start and end apart: 3, of which 3 were waited for; matrix products, arithmetic and copies ran while one was open for 8% of the time, Pallas kernels for 0%

commit v1 on v0

v1 whole, which is shorter than its diff:
```python
import functools

import jax
import jax.numpy as jnp
from jax import lax
from jax.experimental import pallas as pl
from jax.experimental.pallas import tpu as pltpu
from jax.sharding import PartitionSpec as P

LANES = 128
f32 = jnp.float32


def pad_rows(rows):
    return -(-rows // 8) * 8


def source_layers(sd_ref, count, width):
    row = lax.broadcasted_iota(jnp.int32, (count, width), 0)
    layers = jnp.zeros((count, width), jnp.int32)
    for k in range(count):
        layers = jnp.where(row == k, sd_ref[k], layers)
    return layers


def summarize(coef, w, sd, first, obs_ref, lanes):
    nz = coef.shape[0]
    decay = jnp.exp(-coef)
    above = sd < first
    f = jnp.where(above, 1.0, 0.0)
    through = jnp.ones((1, coef.shape[1]), f32)
    squares = jnp.zeros_like(through)
    cross = jnp.zeros_like(w)
    own = jnp.zeros_like(w)
    for z in range(nz):
        step = decay[z : z + 1]
        f = step * f + jnp.where(sd == first + z, w, 0.0)
        through = through * step
        squares = squares + through * through
        cross = cross + f * obs_ref[z, :, lanes]
        own = own + f * f
    rows = jnp.where(above, cross, f)
    part = jnp.where(above, 0.0, own - 2.0 * cross)
    return rows, through, squares, part


def total(x):
    return jnp.sum(jnp.sum(x, axis=0, keepdims=True), axis=1, keepdims=True)


def write_summary(out_ref, n, rows, through, squares):
    k = rows.shape[0]
    out_ref[n, 0:k, :] = rows
    out_ref[n, k : k + 1, :] = through
    out_ref[n, k + 1 : k + 2, :] = squares


def first_kernel(depth_count, sd_ref, model_ref, rate_ref, w_ref, obs_ref, out_ref, energy_ref):
    blocks, width = out_ref.shape[0], out_ref.shape[2]
    nz = model_ref.shape[0]
    sd = source_layers(sd_ref, w_ref.shape[0], width)
    first = lax.axis_index("depth") * nz
    energy = jnp.zeros((1, 1), f32)
    for n in range(blocks):
        lanes = slice(n * width, (n + 1) * width)
        model = model_ref[:, lanes]
        coef = rate_ref[:, lanes] * (1.0 / depth_count) * jnp.exp(0.5 * model)
        rows, through, squares, part = summarize(coef, w_ref[:, lanes], sd, first, obs_ref, lanes)
        write_summary(out_ref, n, rows, through, squares)
        energy = energy + total(part) / w_ref.shape[0] + 0.5 * total(model * model)
    energy_ref[...] = jnp.broadcast_to(energy, energy_ref.shape)


def scan_slabs(sd, nz, got_ref):
    blocks = got_ref.shape[0]
    k = sd.shape[0]
    carry = jnp.zeros(sd.shape, f32)
    energy = jnp.zeros(sd.shape, f32)
    carries = []
    for n in range(blocks):
        rows = got_ref[n, 0:k, :]
        through = got_ref[n, k : k + 1, :]
        squares = got_ref[n, k + 1 : k + 2, :]
        carries.append(carry)
        energy = energy + carry * (carry * squares - 2.0 * rows)
        carry = through * carry + jnp.where(sd >= n * nz, rows, 0.0)
    return carries, energy


def owner_kernel(nz, sd_ref, got_ref, out_ref, energy_ref):
    blocks, _, width = got_ref.shape
    k = sd_ref.shape[0]
    sd = source_layers(sd_ref, k, width)
    carries, energy = scan_slabs(sd, nz, got_ref)
    deeper = jnp.zeros(sd.shape, f32)
    for n in reversed(range(blocks)):
        above = sd < n * nz
        out_ref[n, 0:k, :] = jnp.where(above, carries[n], deeper)
        out_ref[n, k : k + 1, :] = jnp.sum(jnp.where(above, deeper, 0.0), axis=0, keepdims=True)
        rows = got_ref[n, 0:k, :]
        squares = got_ref[n, k + 1 : k + 2, :]
        deeper = deeper + carries[n] * (carries[n] * squares - rows)
    energy_ref[...] = jnp.broadcast_to(total(energy) / k, energy_ref.shape)


def gradient_kernel(
    depth_count, sd_ref, got_ref, model_ref, rate_ref, w_ref, obs_ref, noise_ref, basis_ref,
    gradient_ref, out_ref, sums_ref
):
    blocks, _, width = got_ref.shape
    nz = model_ref.shape[0]
    k = w_ref.shape[0]
    rank = basis_ref.shape[0]
    sd = source_layers(sd_ref, k, width)
    first = lax.axis_index("depth") * nz
    above = sd < first
    for n in range(blocks):
        lanes = slice(n * width, (n + 1) * width)
        model = model_ref[:, lanes]
        coef = rate_ref[:, lanes] * (1.0 / depth_count) * jnp.exp(0.5 * model)
        decay = jnp.exp(-coef)
        w = w_ref[:, lanes]
        entering = got_ref[n, 0:k, :]
        f = jnp.where(above, entering, 0.0)
        products = []
        for z in range(nz):
            f = decay[z : z + 1] * f + jnp.where(sd == first + z, w, 0.0)
            products.append(f * (f - obs_ref[z, :, lanes]))
        deeper = jnp.where(above, 0.0, entering)
        below_sum = got_ref[n, k : k + 1, :]
        for z in reversed(range(nz)):
            deeper = deeper + products[z]
            data = jnp.sum(jnp.where(sd < first + z, deeper, 0.0), axis=0, keepdims=True) + below_sum
            gradient_ref[z : z + 1, lanes] = model[z : z + 1] - coef[z : z + 1] / k * data
    columns = model_ref.shape[1]
    grad = gradient_ref[...].astype(jnp.bfloat16).astype(f32)
    noise = noise_ref[...].astype(jnp.bfloat16).astype(f32)

    def fold(x):
        parts = [x[:, c : c + LANES] for c in range(0, columns, LANES)]
        while len(parts) > 1:
            parts = [a + b for a, b in zip(parts[::2], parts[1::2])] + parts[len(parts) & ~1 :]
        return parts[0]

    def project(step, _):
        for i in range(4):
            r = step * 4 + i
            line = basis_ref[r].astype(f32)
            sums_ref[0, r] = fold(line * grad)
            sums_ref[1, r] = fold(line * noise)
        return 0

    lax.fori_loop(0, rank // 4, project, 0)
    for which in range(2):
        lanesums = jnp.sum(sums_ref[which], axis=1)
        line = jnp.sum(lanesums.T, axis=0, keepdims=True)
        for n in range(blocks):
            out_ref[n, which : which + 1, :] = line


def proposal_kernel(
    depth_count, sd_ref, got_ref, curvature_ref, gradient_ref, model_ref, rate_ref, w_ref, obs_ref,
    noise_ref, basis_ref, proposal_ref, out_ref, energy_ref, mix_ref
):
    blocks, width = out_ref.shape[0], out_ref.shape[2]
    nz, columns = model_ref.shape
    k = w_ref.shape[0]
    rank = basis_ref.shape[0]
    projected = got_ref[0, 0:2, :]
    for n in range(1, blocks):
        projected = projected + got_ref[n, 0:2, :]
    curvature = curvature_ref[...]
    damping = curvature / (1.0 + curvature)
    shrink = 1.0 - 1.0 / jnp.sqrt(1.0 + curvature)
    mix = (damping * projected[0:1] - shrink * projected[1:2]).astype(jnp.bfloat16).astype(f32)
    mix_ref[...] = jnp.broadcast_to(mix, (LANES, rank)).T

    def correct(step, sums):
        for i in range(4):
            r = step * 4 + i
            weight = mix_ref[pl.ds(r, 1), :]
            weight = jnp.broadcast_to(weight, (nz, LANES))
            line = basis_ref[r].astype(f32)
            sums = tuple(
                s + line[:, c * LANES : (c + 1) * LANES] * weight for c, s in enumerate(sums)
            )
        return sums

    zero = jnp.zeros((nz, LANES), f32)
    sums = lax.fori_loop(0, rank // 4, correct, (zero,) * (columns // LANES))
    for c, s in enumerate(sums):
        at = slice(c * LANES, (c + 1) * LANES)
        proposal_ref[:, at] = model_ref[:, at] - gradient_ref[:, at] + noise_ref[:, at] + s

    sd = source_layers(sd_ref, k, width)
    first = lax.axis_index("depth") * nz
    energy = jnp.zeros((1, 1), f32)
    for n in range(blocks):
        lanes = slice(n * width, (n + 1) * width)
        model = proposal_ref[:, lanes]
        coef = rate_ref[:, lanes] * (1.0 / depth_count) * jnp.exp(0.5 * model)
        rows, through, squares, part = summarize(coef, w_ref[:, lanes], sd, first, obs_ref, lanes)
        write_summary(out_ref, n, rows, through, squares)
        energy = energy + total(part) / k + 0.5 * total(model * model)
    energy_ref[...] = jnp.broadcast_to(energy, energy_ref.shape)


def energy_kernel(nz, sd_ref, got_ref, first_ref, owner_ref, next_ref, out_ref):
    blocks, _, width = got_ref.shape
    k = sd_ref.shape[0]
    sd = source_layers(sd_ref, k, width)
    _, energy = scan_slabs(sd, nz, got_ref)
    drop = first_ref[...] + owner_ref[...] - next_ref[...] - total(energy) / k
    for n in range(blocks):
        out_ref[n] = drop


def final_kernel(cells, got_ref, out_ref):
    drop = got_ref[0]
    for n in range(1, got_ref.shape[0]):
        drop = drop + got_ref[n]
    out_ref[...] = drop[0:1, 0:1] / cells


def call(kernel, out_shape, in_smem, *args, scratch=(), flops=1000, out_specs=None):
    vmem = pl.BlockSpec(memory_space=pltpu.VMEM)
    smem = pl.BlockSpec(memory_space=pltpu.SMEM)
    many = isinstance(out_shape, (list, tuple))
    return pl.pallas_call(
        kernel,
        out_shape=out_shape,
        in_specs=[smem if i in in_smem else vmem for i in range(len(args))],
        out_specs=[vmem] * len(out_shape) if many else vmem,
        scratch_shapes=scratch,
        compiler_params=pltpu.CompilerParams(vmem_limit_bytes=24 * 2**20),
        cost_estimate=pl.CostEstimate(flops=flops, bytes_accessed=flops, transcendentals=0),
    )(*args)


def local(model_field, column_rate, wavelets, source_depth, observed, basis, curvature, noise_draw):
    slabs = lax.axis_size("depth")
    nz, columns = model_field.shape
    sources = wavelets.shape[0]
    rank = basis.shape[0]
    depth_count = nz * slabs
    width = columns // slabs
    rate = column_rate.reshape(1, columns)
    bends = curvature.reshape(1, rank)
    struct = jax.ShapeDtypeStruct
    summary = struct((slabs, pad_rows(sources + 2), width), f32)
    scalar = struct((8, LANES), f32)

    def exchange(x):
        return lax.all_to_all(x, "depth", 0, 0)

    sent, energy_first = call(
        functools.partial(first_kernel, depth_count), [summary, scalar], (0,),
        source_depth, model_field, rate, wavelets, observed,
    )
    got = exchange(sent)
    sent, energy_owner = call(
        functools.partial(owner_kernel, nz), [struct((slabs, pad_rows(sources + 1), width), f32), scalar], (0,),
        source_depth, got,
    )
    got = exchange(sent)
    gradient, sent = call(
        functools.partial(gradient_kernel, depth_count),
        [struct((nz, columns), f32), struct((slabs, 8, rank), f32)], (0,),
        source_depth, got, model_field, rate, wavelets, observed, noise_draw, basis,
        scratch=[pltpu.VMEM((2, rank, nz, LANES), f32)],
    )
    got = exchange(sent)
    proposal, sent, energy_next = call(
        functools.partial(proposal_kernel, depth_count),
        [struct((nz, columns), f32), summary, scalar], (0,),
        source_depth, got, bends, gradient, model_field, rate, wavelets, observed, noise_draw, basis,
        scratch=[pltpu.VMEM((rank, LANES), f32)],
    )
    got = exchange(sent)
    sent = call(
        functools.partial(energy_kernel, nz), struct((slabs, 8, LANES), f32), (0,),
        source_depth, got, energy_first, energy_owner, energy_next,
    )
    got = exchange(sent)
    gain = call(functools.partial(final_kernel, depth_count * columns), struct((1, 1), f32), (), got)
    return (proposal, gain.reshape(1))


def solution(mesh):
    in_specs = (
        P(("chain", "depth"), None),
        P("chain"),
        P("chain", None),
        P("chain"),
        P(("chain", "depth"), None, None),
        P("chain", "depth", None),
        P("chain"),
        P(("chain", "depth"), None),
    )
    out_specs = (P(("chain", "depth"), None), P("chain"))
    return jax.shard_map(local, mesh=mesh, in_specs=in_specs, out_specs=out_specs, check_vma=False)
```

time: 243 us -> 79.4 us (0.33)
  blocking collectives: 103 us -> 54.8 us
  waiting for transfers between devices: 36.8 us -> 0 us
  other arithmetic: 36.4 us -> 0 us
  between operations: 19.1 us -> 0.66 us
  matrix products: 17.9 us -> 0 us
  local copies, waits for them, and re-layouts: 28.4 us -> 12.2 us
  Pallas kernels: 0 us -> 11.1 us
    all_gather x2 -> x0, blocking collectives: 63.4 us -> none  [from_gathered(): lax.all_gather(log_block[None], 'depth', axis=0, tiled=True)]
    all_to_all x0 -> x5, blocking collectives: none -> 54.8 us  [exchange(): return lax.all_to_all(x, 'depth', 0, 0)]
    psum x2 -> x0, blocking collectives: 39.3 us -> none  [local(): projected, energy_total = lax.psum((local_proj, energy_now), 'depth')]
    all_gather x3 -> x0, waiting for transfers between devices: 36.8 us -> none  [from_gathered(): lax.all_gather(outgoing[None], 'depth', axis=0, tiled=True)]
    dot_general x2 -> x0, matrix products: 17.9 us -> none  [the longest x1 12.3 us: local(): jnp.dot(mixed, flat_basis, preferred_element_type=jnp.float32)]
    eq x16 -> x0, other arithmetic: 15.1 us -> none  [advance(): source_depth == layer]
    pallas_call x0 -> x6, Pallas kernels: none -> 11.1 us  [call(): pl.pallas_call(kernel, out_shape=out_shape, in_specs=[smem if i in in_sme...]
    dynamic_slice x40 -> x0, local copies, waits for them, and re-layouts: 9.73 us -> none  [march_down(): last, fields = lax.scan(advance, start, (decay, layers))]
  transfers between devices with their start and end apart: 3 -> 0, of which waited for: 3 -> 0; matrix products, arithmetic and copies ran while one was open for 8% -> 0% of each run, Pallas kernels for 0% -> 0%
where the time goes in v1:
time: 79.4 us; the launch traced here: 78.8 us
  blocking collectives  54.8 us (69%)
  local copies, waits for them, and re-layouts  12.2 us (15%)
  Pallas kernels  11.1 us (14%)
    all_to_all x5, blocking collectives, exchange(): return lax.all_to_all(x, 'depth', 0, 0)  54.8 us
    unnamed x26, local copies, waits for them, and re-layouts  12.2 us
    pallas_call x6, Pallas kernels, call(): pl.pallas_call(kernel, out_shape=out_shape, in_specs=[smem if i in in_sme...  11.1 us

profile of v1, /device:TPU:0, one launch (start us, length us, event | category | flops | bytes accessed | tf_op | source)
XLA Modules:
  0.0 78.8 jit_solution(14014533735857863595)
XLA Ops:
  0.6 0.0 copy-start.12
  0.6 0.0 copy-start.2
  0.7 1.2 %copy-done.2 = f32[8,16,2048]{2,1,0:T(8,128)S(1)} copy-done((f32[8,16,2048]{2,1,0:T(8,128)S(1)}, f32[8,16,2048]{2,1,0:T(8,128)}, u32[]{:S(2)}) %copy-start.2) | copy-done | bytes 1048600
  1.9 0.0 copy-start.4
  1.9 0.9 %copy-done.4 = f32[16,2048]{1,0:T(8,128)S(1)} copy-done((f32[16,2048]{1,0:T(8,128)S(1)}, f32[16,2048]{1,0:T(8,128)}, u32[]{:S(2)}) %copy-start.4) | copy-done | bytes 131096
  2.8 0.0 copy-start.6
  2.8 0.8 %copy-done.6 = f32[8,2048]{1,0:T(8,128)S(1)} copy-done((f32[8,2048]{1,0:T(8,128)S(1)}, f32[8,2048]{1,0:T(8,128)}, u32[]{:S(2)}) %copy-start.6) | copy-done | bytes 65560
  3.6 0.0 copy-start.9
  3.6 0.7 copy-done.9
  4.3 0.0 copy-start.11
  4.3 0.7 copy-done.11
  5.0 1.0 %shard_map.95 = (f32[8,24,256]{2,1,0:T(8,128)S(1)}, f32[8,128]{1,0:T(8,128)S(1)}) custom-call(s32[16]{0:T(128)S(1)} %copy-done.11, f32[8,2048]{1,0:T(8,128)S(1)} %copy-done.6, f32[1,2048]{1,0:T(1,128)S(1)} %bitcast.3, f32[16,2048]{1,0:T(8,128)S(1)} %copy-done.4, f32[8,16,2048]{2,1,0:T(8,128)S(1)} %copy-done.2), custom_call_target="tpu_custom_call" | custom-call | flops 1000 | bytes 1000 | tf_op jit(solution)/shard_map/pallas_call | solution.py:229
  6.0 15.1 %all_to_all.25.got_ref = f32[8,24,256]{2,1,0:T(8,128)S(1)} all-to-all(f32[8,24,256]{2,1,0:T(8,128)S(1)} %get-tuple-element.11), channel_id=1, replica_groups=mesh['chain'=4,'depth'=8] {'depth'}, dimensions={0} | all-to-all | bytes 393216 | tf_op jit(solution)/shard_map/all_to_all | solution.py:254
  21.0 0.7 shard_map.96
  21.7 10.7 %all_to_all.26.got_ref = f32[8,24,256]{2,1,0:T(8,128)S(1)} all-to-all(f32[8,24,256]{2,1,0:T(8,128)S(1)} %get-tuple-element.12), channel_id=1, replica_groups=mesh['chain'=4,'depth'=8] {'depth'}, dimensions={0} | all-to-all | bytes 393216 | tf_op jit(solution)/shard_map/all_to_all | solution.py:254
  32.4 0.0 copy-start
  32.4 3.4 %copy-done = bf16[256,8,2048]{2,1,0:T(8,128)(2,1)S(1)} copy-done((bf16[256,8,2048]{2,1,0:T(8,128)(2,1)S(1)}, bf16[256,8,2048]{2,1,0:T(8,128)(2,1)}, u32[]{:S(2)}) %copy-start) | copy-done | bytes 8388632
  35.8 0.0 copy-start.3
  35.8 1.2 %copy-done.3 = f32[8,16,2048]{2,1,0:T(8,128)S(1)} copy-done((f32[8,16,2048]{2,1,0:T(8,128)S(1)}, f32[8,16,2048]{2,1,0:T(8,128)}, u32[]{:S(2)}) %copy-start.3) | copy-done | bytes 1048600
  37.0 0.9 %copy-done.5 = f32[16,2048]{1,0:T(8,128)S(1)} copy-done((f32[16,2048]{1,0:T(8,128)S(1)}, f32[16,2048]{1,0:T(8,128)}, u32[]{:S(2)}) %copy-start.5) | copy-done | bytes 131096
  38.0 0.8 %copy-done.7 = f32[8,2048]{1,0:T(8,128)S(1)} copy-done((f32[8,2048]{1,0:T(8,128)S(1)}, f32[8,2048]{1,0:T(8,128)}, u32[]{:S(2)}) %copy-start.7) | copy-done | bytes 65560
  38.8 0.8 %copy-done.8 = f32[8,2048]{1,0:T(8,128)S(1)} copy-done((f32[8,2048]{1,0:T(8,128)S(1)}, f32[8,2048]{1,0:T(8,128)}, u32[]{:S(2)}) %copy-start.8) | copy-done | bytes 65560
  39.6 0.7 copy-done.10
  40.3 4.7 %shard_map.97 = (f32[8,2048]{1,0:T(8,128)S(1)}, f32[8,8,256]{2,1,0:T(8,128)S(1)}) custom-call(s32[16]{0:T(128)S(1)} %copy-done.11, f32[8,24,256]{2,1,0:T(8,128)S(1)} %all_to_all.26.got_ref, f32[8,2048]{1,0:T(8,128)S(1)} %copy-done.7, f32[1,2048]{1,0:T(1,128)S(1)} %bitcast.4, f32[16,2048]{1,0:T(8,128)S(1)} %copy-done.5, f32[8,16,2048]{2,1,0:T(8,128)S(1)} %copy-done.3, ...), custom_call_target="tpu_custom_call" | custom-call | flops 1000 | bytes 1000 | tf_op jit(solution)/shard_map/pallas_call | solution.py:229
  45.0 9.8 %all_to_all.27.got_ref = f32[8,8,256]{2,1,0:T(8,128)S(1)} all-to-all(f32[8,8,256]{2,1,0:T(8,128)S(1)} %get-tuple-element.13), channel_id=1, replica_groups=mesh['chain'=4,'depth'=8] {'depth'}, dimensions={0} | all-to-all | bytes 131072 | tf_op jit(solution)/shard_map/all_to_all | solution.py:254
  54.8 0.0 copy-done.12
  54.8 0.0 copy-done.1
  54.8 3.6 %shard_map.98 = (f32[8,2048]{1,0:T(8,128)}, f32[8,24,256]{2,1,0:T(8,128)S(1)}, f32[8,128]{1,0:T(8,128)S(1)}) custom-call(s32[16]{0:T(128)S(1)} %copy-done.11, f32[8,8,256]{2,1,0:T(8,128)S(1)} %all_to_all.27.got_ref, f32[1,256]{1,0:T(1,128)S(1)} %bitcast.6, f32[8,2048]{1,0:T(8,128)S(1)} %get-tuple-element.14.gradient_ref, f32[8,2048]{1,0:T(8,128)S(1)} %copy-done.7, ...), custom_call_target="tpu_custom_call" | custom-call | flops 1000 | bytes 1000 | tf_op jit(solution)/shard_map/pallas_call | solution.py:229
  58.3 10.2 %all_to_all.28.got_ref = f32[8,24,256]{2,1,0:T(8,128)S(1)} all-to-all(f32[8,24,256]{2,1,0:T(8,128)S(1)} %get-tuple-element.16), channel_id=1, replica_groups=mesh['chain'=4,'depth'=8] {'depth'}, dimensions={0} | all-to-all | bytes 393216 | tf_op jit(solution)/shard_map/all_to_all | solution.py:254
  68.5 0.7 shard_map.99
  69.2 9.1 %all_to_all.29.got_ref = f32[8,8,128]{2,1,0:T(8,128)S(1)} all-to-all(f32[8,8,128]{2,1,0:T(8,128)S(1)} %shard_map.99), channel_id=1, replica_groups=mesh['chain'=4,'depth'=8] {'depth'}, dimensions={0} | all-to-all | bytes 65536 | tf_op jit(solution)/shard_map/all_to_all | solution.py:254
  78.3 0.5 shard_map.100
  (5 shorter events, 0.0 us)
Async XLA Ops:
  0.6 54.1 %copy-start.12 = (f32[256]{0:T(256)S(1)}, f32[256]{0:T(256)}, u32[]{:S(2)}) copy-start(f32[256]{0:T(256)} %param.14) | copy-start | bytes 3076
  0.6 1.2 %copy-start.2 = (f32[8,16,2048]{2,1,0:T(8,128)S(1)}, f32[8,16,2048]{2,1,0:T(8,128)}, u32[]{:S(2)}) copy-start(f32[8,16,2048]{2,1,0:T(8,128)} %obs_ref.5) | copy-start | bytes 3145732
  1.9 0.9 %copy-start.4 = (f32[16,2048]{1,0:T(8,128)S(1)}, f32[16,2048]{1,0:T(8,128)}, u32[]{:S(2)}) copy-start(f32[16,2048]{1,0:T(8,128)} %w_ref.5) | copy-start | bytes 393220
  2.8 0.8 %copy-start.6 = (f32[8,2048]{1,0:T(8,128)S(1)}, f32[8,2048]{1,0:T(8,128)}, u32[]{:S(2)}) copy-start(f32[8,2048]{1,0:T(8,128)} %model_ref.5) | copy-start | bytes 196612
  3.6 0.7 copy-start.9
  4.3 0.7 copy-start.11
  32.4 3.4 %copy-start = (bf16[256,8,2048]{2,1,0:T(8,128)(2,1)S(1)}, bf16[256,8,2048]{2,1,0:T(8,128)(2,1)}, u32[]{:S(2)}) copy-start(bf16[256,8,2048]{2,1,0:T(8,128)(2,1)} %basis_ref.3) | copy-start | bytes 25165828
  35.8 1.2 %copy-start.3 = (f32[8,16,2048]{2,1,0:T(8,128)S(1)}, f32[8,16,2048]{2,1,0:T(8,128)}, u32[]{:S(2)}) copy-start(f32[8,16,2048]{2,1,0:T(8,128)} %obs_ref.5) | copy-start | bytes 3145732
  37.0 0.9 %copy-start.5 = (f32[16,2048]{1,0:T(8,128)S(1)}, f32[16,2048]{1,0:T(8,128)}, u32[]{:S(2)}) copy-start(f32[16,2048]{1,0:T(8,128)} %w_ref.5) | copy-start | bytes 393220
  37.9 0.8 %copy-start.7 = (f32[8,2048]{1,0:T(8,128)S(1)}, f32[8,2048]{1,0:T(8,128)}, u32[]{:S(2)}) copy-start(f32[8,2048]{1,0:T(8,128)} %model_ref.5) | copy-start | bytes 196612
  38.8 0.8 %copy-start.8 = (f32[8,2048]{1,0:T(8,128)S(1)}, f32[8,2048]{1,0:T(8,128)}, u32[]{:S(2)}) copy-start(f32[8,2048]{1,0:T(8,128)} %noise_ref.3) | copy-start | bytes 196612
  39.6 0.7 copy-start.10
  40.3 14.4 %copy-start.1 = (bf16[256,8,2048]{2,1,0:T(8,128)(2,1)S(1)}, bf16[256,8,2048]{2,1,0:T(8,128)(2,1)}, u32[]{:S(2)}) copy-start(bf16[256,8,2048]{2,1,0:T(8,128)(2,1)} %basis_ref.3) | copy-start | bytes 25165828

commit v2 on v1

v2 whole, which is shorter than its diff:
```python
import functools

import jax
import jax.numpy as jnp
from jax import lax
from jax.experimental import pallas as pl
from jax.experimental.pallas import tpu as pltpu
from jax.sharding import PartitionSpec as P

LANES = 128
f32 = jnp.float32


def pad_rows(rows):
    return -(-rows // 8) * 8


def source_layers(sd_ref, count):
    row = lax.broadcasted_iota(jnp.int32, (count, LANES), 0)
    layers = jnp.zeros((count, LANES), jnp.int32)
    for k in range(count):
        layers = jnp.where(row == k, sd_ref[k], layers)
    return layers


def widen(layers_ref, width):
    layers = layers_ref[...]
    if width % LANES == 0:
        return jnp.concatenate([layers] * (width // LANES), axis=1)
    return layers[:, :width]


def split(width):
    return (width // LANES, LANES) if width % LANES == 0 else (1, width)


def wide(ref, n, start, count, parts):
    pieces = [ref[n, parts * start + p * count : parts * start + (p + 1) * count, :] for p in range(parts)]
    return pieces[0] if parts == 1 else jnp.concatenate(pieces, axis=1)


def put_wide(ref, n, start, value, parts):
    count, lanes = value.shape[0], value.shape[1] // parts
    for p in range(parts):
        ref[n, parts * start + p * count : parts * start + (p + 1) * count, :] = value[:, p * lanes : (p + 1) * lanes]


def summarize(coef, w, sd, first, obs_ref, lanes):
    nz = coef.shape[0]
    decay = jnp.exp(-coef)
    above = sd < first
    f = jnp.where(above, 1.0, 0.0)
    through = jnp.ones((1, coef.shape[1]), f32)
    squares = jnp.zeros_like(through)
    cross = jnp.zeros_like(w)
    own = jnp.zeros_like(w)
    for z in range(nz):
        step = decay[z : z + 1]
        f = step * f + jnp.where(sd == first + z, w, 0.0)
        through = through * step
        squares = squares + through * through
        cross = cross + f * obs_ref[z, :, lanes]
        own = own + f * f
    rows = jnp.where(above, cross, f)
    part = jnp.where(above, 0.0, own - 2.0 * cross)
    return rows, through, squares, part


def total(x):
    return jnp.sum(jnp.sum(x, axis=0, keepdims=True), axis=1, keepdims=True)


def write_summary(out_ref, n, rows, through, squares, parts):
    k = rows.shape[0]
    put_wide(out_ref, n, 0, rows, parts)
    put_wide(out_ref, n, k, through, parts)
    put_wide(out_ref, n, k + 1, squares, parts)


def first_kernel(
    depth_count, blocks, sd_hbm, model_hbm, rate_hbm, w_hbm, obs_hbm, noise_hbm, curvature_hbm,
    out_ref, energy_ref, layers_ref, model_ref, rate_ref, w_ref, obs_ref, noise_ref, curvature_ref,
    sd_ref, sems, obs_sems
):
    nz, columns = model_ref.shape
    k = w_ref.shape[0]
    width = columns // blocks
    parts = split(width)[0]
    copies = [
        pltpu.make_async_copy(src, dst, sems.at[i])
        for i, (src, dst) in enumerate([
            (sd_hbm, sd_ref), (model_hbm, model_ref), (rate_hbm, rate_ref), (w_hbm, w_ref),
            (noise_hbm, noise_ref), (curvature_hbm, curvature_ref),
        ])
    ]
    pieces = obs_sems.shape[0]
    piece = columns // pieces
    obs_copies = []
    for i in range(pieces):
        at = pl.ds(i * piece, piece)
        obs_copies.append(pltpu.make_async_copy(obs_hbm.at[:, :, at], obs_ref.at[:, :, at], obs_sems.at[i]))
    for copy in copies[:4]:
        copy.start()
    for copy in obs_copies:
        copy.start()
    for copy in copies[4:]:
        copy.start()
    for copy in copies[:4]:
        copy.wait()
    layers_ref[...] = source_layers(sd_ref, k)
    sd = widen(layers_ref, width)
    first = lax.axis_index("depth") * nz
    energy = jnp.zeros((1, 1), f32)
    arrived = 0
    for n in range(blocks):
        while arrived * piece < (n + 1) * width:
            obs_copies[arrived].wait()
            arrived += 1
        lanes = slice(n * width, (n + 1) * width)
        model = model_ref[:, lanes]
        coef = rate_ref[:, lanes] * (1.0 / depth_count) * jnp.exp(0.5 * model)
        rows, through, squares, part = summarize(coef, w_ref[:, lanes], sd, first, obs_ref, lanes)
        write_summary(out_ref, n, rows, through, squares, parts)
        energy = energy + total(part) / k + 0.5 * total(model * model)
    energy_ref[...] = jnp.broadcast_to(energy, energy_ref.shape)
    for copy in copies[4:]:
        copy.wait()


def project(vectors, basis_ref, rows, full_ref):
    full_ref[rows, :] = lax.dot_general(
        basis_ref[rows, :], vectors, (((1,), (1,)), ((), ())), preferred_element_type=f32
    )


def directions(full_ref, nz):
    rank = full_ref.shape[0] // nz
    lane = lax.broadcasted_iota(jnp.int32, (rank, nz), 1)
    picked = jnp.zeros((rank, nz), f32)
    for z in range(nz):
        picked = jnp.where(lane == z, full_ref[pl.ds(z, rank, stride=nz), :], picked)
    ones = jnp.ones((8, nz), f32)
    return lax.dot_general(
        ones, picked, (((1,), (1,)), ((), ())), precision=lax.Precision.HIGHEST, preferred_element_type=f32
    )[0:1]


def stream(basis_hbm, basis_ref, sems):
    pieces = sems.shape[0]
    piece = basis_ref.shape[0] // pieces
    started = []
    for i in range(pieces):
        rows = pl.ds(i * piece, piece)
        copy = pltpu.make_async_copy(basis_hbm.at[rows, :], basis_ref.at[rows, :], sems.at[i])
        copy.start()
        started.append((rows, copy))
    return started


def noise_kernel(nz, basis_hbm, noise_ref, q_ref, basis_ref, full_ref, sems):
    vectors = noise_ref[...].astype(jnp.bfloat16)
    for rows, copy in stream(basis_hbm, basis_ref, sems):
        copy.wait()
        project(vectors, basis_ref, rows, full_ref)
    q_ref[...] = directions(full_ref, nz)


def scan_slabs(sd, nz, got_ref, parts):
    blocks = got_ref.shape[0]
    k = sd.shape[0]
    carry = jnp.zeros(sd.shape, f32)
    energy = jnp.zeros(sd.shape, f32)
    carries = []
    for n in range(blocks):
        rows = wide(got_ref, n, 0, k, parts)
        through = wide(got_ref, n, k, 1, parts)
        squares = wide(got_ref, n, k + 1, 1, parts)
        carries.append(carry)
        energy = energy + carry * (carry * squares - 2.0 * rows)
        carry = through * carry + jnp.where(sd >= n * nz, rows, 0.0)
    return carries, energy


def owner_kernel(nz, width, layers_ref, got_ref, out_ref, energy_ref):
    blocks = got_ref.shape[0]
    parts = split(width)[0]
    k = layers_ref.shape[0]
    sd = widen(layers_ref, width)
    carries, energy = scan_slabs(sd, nz, got_ref, parts)
    deeper = jnp.zeros(sd.shape, f32)
    for n in reversed(range(blocks)):
        above = sd < n * nz
        put_wide(out_ref, n, 0, jnp.where(above, carries[n], deeper), parts)
        put_wide(out_ref, n, k, jnp.sum(jnp.where(above, deeper, 0.0), axis=0, keepdims=True), parts)
        rows = wide(got_ref, n, 0, k, parts)
        squares = wide(got_ref, n, k + 1, 1, parts)
        deeper = deeper + carries[n] * (carries[n] * squares - rows)
    energy_ref[...] = jnp.broadcast_to(total(energy) / k, energy_ref.shape)


def gradient_kernel(
    depth_count, layers_ref, got_ref, model_ref, rate_ref, w_ref, obs_ref, q_ref, basis_hbm,
    gradient_ref, out_ref, basis_ref, spread_ref, full_ref, sems
):
    started = stream(basis_hbm, basis_ref, sems)
    blocks = got_ref.shape[0]
    nz, columns = model_ref.shape
    width = columns // blocks
    parts = split(width)[0]
    k = w_ref.shape[0]
    sd = widen(layers_ref, width)
    first = lax.axis_index("depth") * nz
    above = sd < first
    for n in range(blocks):
        lanes = slice(n * width, (n + 1) * width)
        model = model_ref[:, lanes]
        coef = rate_ref[:, lanes] * (1.0 / depth_count) * jnp.exp(0.5 * model)
        decay = jnp.exp(-coef)
        w = w_ref[:, lanes]
        entering = wide(got_ref, n, 0, k, parts)
        f = jnp.where(above, entering, 0.0)
        products = []
        for z in range(nz):
            f = decay[z : z + 1] * f + jnp.where(sd == first + z, w, 0.0)
            products.append(f * (f - obs_ref[z, :, lanes]))
        deeper = jnp.where(above, 0.0, entering)
        below_sum = wide(got_ref, n, k, 1, parts)
        for z in reversed(range(nz)):
            deeper = deeper + products[z]
            data = jnp.sum(jnp.where(sd < first + z, deeper, 0.0), axis=0, keepdims=True) + below_sum
            gradient_ref[z : z + 1, lanes] = model[z : z + 1] - coef[z : z + 1] / k * data
    row = lax.broadcasted_iota(jnp.int32, spread_ref.shape, 0)
    column = lax.broadcasted_iota(jnp.int32, spread_ref.shape, 1)
    spread_ref[...] = jnp.where(row == column // nz, 1.0, 0.0).astype(jnp.bfloat16)
    vectors = gradient_ref[...].astype(jnp.bfloat16)
    for rows, copy in started:
        copy.wait()
        project(vectors, basis_ref, rows, full_ref)
    line = directions(full_ref, nz)
    for n in range(blocks):
        out_ref[n, 0:1, :] = line
        out_ref[n, 1:2, :] = q_ref[...]


def proposal_kernel(
    depth_count, width, layers_ref, got_ref, curvature_ref, gradient_ref, model_ref, rate_ref, w_ref,
    obs_ref, noise_ref, basis_ref, spread_ref, proposal_ref, out_ref, energy_ref
):
    blocks = out_ref.shape[0]
    parts = split(width)[0]
    nz, columns = model_ref.shape
    k = w_ref.shape[0]
    rank, total_rows = spread_ref.shape
    projected = got_ref[0, 0:2, :]
    for n in range(1, blocks):
        projected = projected + got_ref[n, 0:2, :]
    curvature = curvature_ref[...]
    damping = curvature / (1.0 + curvature)
    shrink = 1.0 - 1.0 / jnp.sqrt(1.0 + curvature)
    mix = (damping * projected[0:1] - shrink * projected[1:2]).astype(jnp.bfloat16)
    spread = jnp.dot(jnp.broadcast_to(mix, (nz, rank)), spread_ref[...], preferred_element_type=f32)
    row = lax.broadcasted_iota(jnp.int32, (nz, total_rows), 0)
    column = lax.broadcasted_iota(jnp.int32, (nz, total_rows), 1)
    weights = jnp.where(row == column % nz, spread, 0.0).astype(jnp.bfloat16)
    correction = jnp.dot(weights, basis_ref[...], preferred_element_type=f32)
    proposal_ref[...] = model_ref[...] - gradient_ref[...] + noise_ref[...] + correction

    sd = widen(layers_ref, width)
    first = lax.axis_index("depth") * nz
    energy = jnp.zeros((1, 1), f32)
    for n in range(blocks):
        lanes = slice(n * width, (n + 1) * width)
        model = proposal_ref[:, lanes]
        coef = rate_ref[:, lanes] * (1.0 / depth_count) * jnp.exp(0.5 * model)
        rows, through, squares, part = summarize(coef, w_ref[:, lanes], sd, first, obs_ref, lanes)
        write_summary(out_ref, n, rows, through, squares, parts)
        energy = energy + total(part) / k + 0.5 * total(model * model)
    energy_ref[...] = jnp.broadcast_to(energy, energy_ref.shape)


def energy_kernel(nz, width, layers_ref, got_ref, first_ref, owner_ref, next_ref, out_ref):
    blocks = got_ref.shape[0]
    k = layers_ref.shape[0]
    sd = widen(layers_ref, width)
    _, energy = scan_slabs(sd, nz, got_ref, split(width)[0])
    drop = first_ref[...] + owner_ref[...] - next_ref[...] - total(energy) / k
    for n in range(blocks):
        out_ref[n] = drop


def final_kernel(cells, got_ref, out_ref):
    drop = got_ref[0]
    for n in range(1, got_ref.shape[0]):
        drop = drop + got_ref[n]
    out_ref[...] = drop[0:1, 0:1] / cells


def call(kernel, outs, args, hbm=(), scratch=(), flops=10**6, limit=16):
    vmem = pl.BlockSpec(memory_space=pltpu.VMEM)
    far = pl.BlockSpec(memory_space=pltpu.HBM)
    args = [pltpu.with_memory_space_constraint(x, pltpu.HBM) if i in hbm else x for i, x in enumerate(args)]
    return pl.pallas_call(
        kernel,
        out_shape=outs,
        in_specs=[far if i in hbm else vmem for i in range(len(args))],
        out_specs=[vmem] * len(outs),
        scratch_shapes=scratch,
        compiler_params=pltpu.CompilerParams(vmem_limit_bytes=limit * 2**20),
        cost_estimate=pl.CostEstimate(flops=flops, bytes_accessed=flops, transcendentals=0),
    )(*args)


def local(model_field, column_rate, wavelets, source_depth, observed, basis, curvature, noise_draw):
    slabs = lax.axis_size("depth")
    nz, columns = model_field.shape
    sources = wavelets.shape[0]
    rank = basis.shape[0]
    depth_count = nz * slabs
    width = columns // slabs
    parts, lanes = split(width)
    struct = jax.ShapeDtypeStruct
    summary = struct((slabs, pad_rows(parts * (sources + 2)), lanes), f32)
    answer = struct((slabs, pad_rows(parts * (sources + 1)), lanes), f32)
    scalar = struct((8, LANES), f32)
    field = struct((nz, columns), f32)
    dma = pltpu.SemaphoreType.DMA

    def exchange(x):
        return lax.all_to_all(x, "depth", 0, 0)

    sent, energy_first, layers, model, rate, w, obs, noise, bends = call(
        functools.partial(first_kernel, depth_count, slabs),
        [summary, scalar, struct((sources, LANES), jnp.int32), field, struct((1, columns), f32),
         struct(wavelets.shape, f32), struct(observed.shape, f32), field, struct((1, rank), f32)],
        [source_depth, model_field, column_rate.reshape(1, columns), wavelets, observed, noise_draw,
         curvature.reshape(1, rank)],
        hbm=range(7),
        scratch=[pltpu.SMEM((sources,), jnp.int32), dma((6,)), dma((8,))],
    )
    got = exchange(sent)
    flat = basis.reshape(rank * nz, columns)
    buffers = [pltpu.VMEM((rank * nz, nz), f32), dma((8,))]
    (q,) = call(
        functools.partial(noise_kernel, nz), [struct((1, rank), f32)], [flat, noise], hbm=(0,),
        scratch=[pltpu.VMEM(flat.shape, flat.dtype)] + buffers, flops=10**8, limit=24,
    )
    sent, energy_owner = call(
        functools.partial(owner_kernel, nz, width), [answer, scalar], [layers, got],
    )
    got = exchange(sent)
    gradient, sent, near, spread = call(
        functools.partial(gradient_kernel, depth_count),
        [field, struct((slabs, 8, rank), f32), struct(flat.shape, flat.dtype),
         struct((rank, rank * nz), jnp.bfloat16)],
        [layers, got, model, rate, w, obs, q, flat], hbm=(7,), scratch=buffers, limit=24,
    )
    got = exchange(sent)
    proposal, sent, energy_next = call(
        functools.partial(proposal_kernel, depth_count, width),
        [field, summary, scalar],
        [layers, got, bends, gradient, model, rate, w, obs, noise, near, spread], limit=24,
    )
    got = exchange(sent)
    (sent,) = call(
        functools.partial(energy_kernel, nz, width), [struct((slabs, 8, LANES), f32)],
        [layers, got, energy_first, energy_owner, energy_next],
    )
    got = exchange(sent)
    (gain,) = call(functools.partial(final_kernel, depth_count * columns), [struct((1, 1), f32)], [got])
    return (proposal, gain.reshape(1))


def solution(mesh):
    in_specs = (
        P(("chain", "depth"), None),
        P("chain"),
        P("chain", None),
        P("chain"),
        P(("chain", "depth"), None, None),
        P("chain", "depth", None),
        P("chain"),
        P(("chain", "depth"), None),
    )
    out_specs = (P(("chain", "depth"), None), P("chain"))
    return jax.shard_map(local, mesh=mesh, in_specs=in_specs, out_specs=out_specs, check_vma=False)
```

time: 79.4 us -> 70.4 us (0.89)
  local copies, waits for them, and re-layouts: 12.2 us -> 0 us
  blocking collectives: 54.8 us -> 45.6 us
  Pallas kernels: 11.1 us -> 19.7 us
  starting transfers between devices: 0 us -> 3.38 us
    unnamed x26 -> x0, local copies, waits for them, and re-layouts: 12.2 us -> none
    all_to_all x5 -> x4, blocking collectives: 54.8 us -> 45.6 us  [exchange(): return lax.all_to_all(x, 'depth', 0, 0)]
    pallas_call x6 -> x7, Pallas kernels: 11.1 us -> 19.7 us  [call(): pl.pallas_call(kernel, out_shape=outs, in_specs=[far if i in hbm else vme...]
    all_to_all x0 -> x1, starting transfers between devices: none -> 3.38 us  [exchange(): return lax.all_to_all(x, 'depth', 0, 0)]
  transfers between devices with their start and end apart: 0 -> 1, of which waited for: 0 -> 1; matrix products, arithmetic and copies ran while one was open for 0% -> 0% of each run, Pallas kernels for 0% -> 10%
where the time goes in v2:
time: 70.4 us; the launch traced here: 70 us
  blocking collectives  45.6 us (65%)
  Pallas kernels  19.7 us (28%)
  starting transfers between devices  3.38 us (5%)
    all_to_all x4, blocking collectives, exchange(): return lax.all_to_all(x, 'depth', 0, 0)  45.6 us
    pallas_call x7, Pallas kernels, call(): pl.pallas_call(kernel, out_shape=outs, in_specs=[far if i in hbm else vme...  19.7 us
    all_to_all x1, starting transfers between devices, exchange(): return lax.all_to_all(x, 'depth', 0, 0)  3.38 us
  transfers between devices with their start and end apart: 1, of which 1 were waited for; matrix products, arithmetic and copies ran while one was open for 0% of the time, Pallas kernels for 10%

profile of v2, /device:TPU:0, one launch (start us, length us, event | category | flops | bytes accessed | tf_op | source)
XLA Modules:
  0.0 70.0 jit_solution(12126511961044593863)
XLA Ops:
  0.6 2.5 %shard_map.95 = (f32[8,40,128]{2,1,0:T(8,128)S(1)}, f32[8,128]{1,0:T(8,128)S(1)}, s32[16,128]{1,0:T(8,128)S(1)}, f32[8,2048]{1,0:T(8,128)S(1)}, f32[1,2048]{1,0:...) custom-call(s32[16]{0:T(128)} %sd_hbm.1, ...), custom_call_target="tpu_custom_call" | custom-call | flops 1000000 | bytes 1000000 | tf_op jit(solution)/shard_map/pallas_call | solution.py:302
  3.2 14.7 %all_to_all.25.got_ref = f32[8,40,128]{2,1,0:T(8,128)S(1)} all-to-all(f32[8,40,128]{2,1,0:T(8,128)S(1)} %get-tuple-element.21), channel_id=1, replica_groups=mesh['chain'=4,'depth'=8] {'depth'}, dimensions={0} | all-to-all | bytes 327680 | tf_op jit(solution)/shard_map/all_to_all | solution.py:329
  17.8 0.7 %shard_map.96 = (f32[8,40,128]{2,1,0:T(8,128)}, f32[8,128]{1,0:T(8,128)S(1)}) custom-call(s32[16,128]{1,0:T(8,128)S(1)} %get-tuple-element.20.layers_ref, f32[8,40,128]{2,1,0:T(8,128)S(1)} %all_to_all.25.got_ref), custom_call_target="tpu_custom_call" | custom-call | flops 1000000 | bytes 1000000 | tf_op jit(solution)/shard_map/pallas_call | solution.py:302
  18.6 3.4 %all-to-all-start.1 = ((f32[8,40,128]{2,1,0:T(8,128)}), f32[8,40,128]{2,1,0:T(8,128)S(1)}, u32[]{:S(2)}, u32[]{:S(2)}) async-start(f32[8,40,128]{2,1,0:T(8,128)} %get-tuple-element.22), calls=%async_computation.1 | async-start | bytes 327680 | tf_op jit(solution)/shard_map/all_to_all | solution.py:329
  22.0 6.8 %shard_map.97.q_ref = f32[1,256]{1,0:T(1,128)S(1)} custom-call(bf16[2048,2048]{1,0:T(8,128)(2,1)} %bitcast.4, f32[8,2048]{1,0:T(8,128)S(1)} %get-tuple-element.27.noise_ref), custom_call_target="tpu_custom_call" | custom-call | flops 100000000 | bytes 100000000 | tf_op jit(solution)/shard_map/pallas_call | solution.py:302
  28.8 0.7 all-to-all-done.1.got_ref
  29.5 6.8 %shard_map.98 = (f32[8,2048]{1,0:T(8,128)S(1)}, f32[8,8,256]{2,1,0:T(8,128)S(1)}, bf16[2048,2048]{1,0:T(8,128)(2,1)S(1)}, bf16[256,2048]{1,0:T(8,128)(2,1)S(1)}) custom-call(s32[16,128]{1,0:T(8,128)S(1)} %get-tuple-element.20.layers_ref, f32[8,40,128]{2,1,0:T(8,128)S(1)} %all-to-all-done.1.got_ref, f32[8,2048]{1,0:T(8,128)S(1)} %get-tuple-element.23.model_ref, ...), custom_call_target="tpu_custom_call" | custom-call | flops 1000000 | bytes 1000000 | tf_op jit(solution)/shard_map/pallas_call | solution.py:302
  36.3 12.0 %all_to_all.26.got_ref = f32[8,8,256]{2,1,0:T(8,128)S(1)} all-to-all(f32[8,8,256]{2,1,0:T(8,128)S(1)} %get-tuple-element.28), channel_id=1, replica_groups=mesh['chain'=4,'depth'=8] {'depth'}, dimensions={0} | all-to-all | bytes 131072 | tf_op jit(solution)/shard_map/all_to_all | solution.py:329
  48.2 2.2 %shard_map.99 = (f32[8,2048]{1,0:T(8,128)}, f32[8,40,128]{2,1,0:T(8,128)S(1)}, f32[8,128]{1,0:T(8,128)S(1)}) custom-call(s32[16,128]{1,0:T(8,128)S(1)} %get-tuple-element.20.layers_ref, f32[8,8,256]{2,1,0:T(8,128)S(1)} %all_to_all.26.got_ref, f32[1,256]{1,0:T(1,128)S(1)} %get-tuple-element.29.curvature_ref, f32[8,2048]{1,0:T(8,128)S(1)} %get-tuple-element.30.gradient_ref, ...), custom_call_target="tpu_custom_call" | custom-call | flops 1000000 | bytes 1000000 | tf_op jit(solution)/shard_map/pallas_call | solution.py:302
  50.4 9.9 %all_to_all.27.got_ref = f32[8,40,128]{2,1,0:T(8,128)S(1)} all-to-all(f32[8,40,128]{2,1,0:T(8,128)S(1)} %get-tuple-element.34), channel_id=1, replica_groups=mesh['chain'=4,'depth'=8] {'depth'}, dimensions={0} | all-to-all | bytes 327680 | tf_op jit(solution)/shard_map/all_to_all | solution.py:329
  60.3 0.1 shard_map.100
  60.5 9.0 %all_to_all.28.got_ref = f32[8,8,128]{2,1,0:T(8,128)S(1)} all-to-all(f32[8,8,128]{2,1,0:T(8,128)S(1)} %shard_map.100), channel_id=1, replica_groups=mesh['chain'=4,'depth'=8] {'depth'}, dimensions={0} | all-to-all | bytes 65536 | tf_op jit(solution)/shard_map/all_to_all | solution.py:329
  69.5 0.5 shard_map.101
Async XLA Ops:
  18.6 10.9 %all-to-all-start.1 = ((f32[8,40,128]{2,1,0:T(8,128)}), f32[8,40,128]{2,1,0:T(8,128)S(1)}, u32[]{:S(2)}, u32[]{:S(2)}) async-start(f32[8,40,128]{2,1,0:T(8,128)} %get-tuple-element.22), calls=%async_computation.1 | async-start | bytes 327680 | tf_op jit(solution)/shard_map/all_to_all | solution.py:329

commit v3 on v2

--- a/solution.py
+++ b/solution.py
@@ -110,59 +110,72 @@
     layers_ref[...] = source_layers(sd_ref, k)
     sd = widen(layers_ref, width)
     first = lax.axis_index("depth") * nz
-    energy = jnp.zeros((1, 1), f32)
-    arrived = 0
-    for n in range(blocks):
-        while arrived * piece < (n + 1) * width:
-            obs_copies[arrived].wait()
-            arrived += 1
+    for copy in obs_copies:
+        copy.wait()
+    misfit = jnp.zeros(sd.shape, f32)
+    square = jnp.zeros((nz, width), f32)
+    for n in range(blocks):
         lanes = slice(n * width, (n + 1) * width)
         model = model_ref[:, lanes]
         coef = rate_ref[:, lanes] * (1.0 / depth_count) * jnp.exp(0.5 * model)
         rows, through, squares, part = summarize(coef, w_ref[:, lanes], sd, first, obs_ref, lanes)
         write_summary(out_ref, n, rows, through, squares, parts)
-        energy = energy + total(part) / k + 0.5 * total(model * model)
-    energy_ref[...] = jnp.broadcast_to(energy, energy_ref.shape)
+        misfit = misfit + part
+        square = square + model * model
+    energy_ref[...] = jnp.broadcast_to(total(misfit) / k + 0.5 * total(square), energy_ref.shape)
     for copy in copies[4:]:
         copy.wait()
 
 
-def project(vectors, basis_ref, rows, full_ref):
-    full_ref[rows, :] = lax.dot_general(
-        basis_ref[rows, :], vectors, (((1,), (1,)), ((), ())), preferred_element_type=f32
-    )
-
-
-def directions(full_ref, nz):
-    rank = full_ref.shape[0] // nz
-    lane = lax.broadcasted_iota(jnp.int32, (rank, nz), 1)
-    picked = jnp.zeros((rank, nz), f32)
-    for z in range(nz):
-        picked = jnp.where(lane == z, full_ref[pl.ds(z, rank, stride=nz), :], picked)
-    ones = jnp.ones((8, nz), f32)
-    return lax.dot_general(
-        ones, picked, (((1,), (1,)), ((), ())), precision=lax.Precision.HIGHEST, preferred_element_type=f32
-    )[0:1]
+def group(nz, offset, expand):
+    one = lax.broadcasted_iota(jnp.int32, (LANES, LANES), 1 - expand)
+    each = lax.broadcasted_iota(jnp.int32, (LANES, LANES), expand)
+    return jnp.where(one == each // nz + offset, 1.0, 0.0)
+
+
+def exact_dot(a, b):
+    return jnp.dot(a, b, precision=lax.Precision.HIGHEST, preferred_element_type=f32)
+
+
+def project(vectors, basis_ref):
+    return lax.dot_general(vectors, basis_ref, (((1,), (1,)), ((), ())), preferred_element_type=f32)
+
+
+def own_layer(every, sums_ref):
+    nz = every.shape[0]
+    layer = lax.broadcasted_iota(jnp.int32, (nz, LANES), 0)
+    lane = lax.broadcasted_iota(jnp.int32, (nz, LANES), 1)
+    for t in range(every.shape[1] // LANES):
+        mine = jnp.where(layer == lane % nz, every[:, t * LANES : (t + 1) * LANES], 0.0)
+        sums_ref[t : t + 1, :] = jnp.sum(mine, axis=0, keepdims=True)
 
 
 def stream(basis_hbm, basis_ref, sems):
     pieces = sems.shape[0]
-    piece = basis_ref.shape[0] // pieces
+    piece = basis_ref.shape[1] // pieces
     started = []
     for i in range(pieces):
-        rows = pl.ds(i * piece, piece)
-        copy = pltpu.make_async_copy(basis_hbm.at[rows, :], basis_ref.at[rows, :], sems.at[i])
+        at = pl.ds(i * piece, piece)
+        copy = pltpu.make_async_copy(basis_hbm.at[:, at], basis_ref.at[:, at], sems.at[i])
         copy.start()
-        started.append((rows, copy))
+        started.append((slice(i * piece, (i + 1) * piece), copy))
     return started
 
 
-def noise_kernel(nz, basis_hbm, noise_ref, q_ref, basis_ref, full_ref, sems):
+def noise_kernel(nz, basis_hbm, noise_ref, curvature_ref, q_ref, bends_ref, basis_ref, sums_ref, sems):
+    started = stream(basis_hbm, basis_ref, sems)
+    share = LANES // nz
+    sums_ref[...] = jnp.zeros_like(sums_ref)
+    for i in range(sums_ref.shape[0]):
+        sums_ref[i : i + 1, 0:share] = curvature_ref[:, i * share : (i + 1) * share]
+    bends_ref[...] = exact_dot(sums_ref[...], group(nz, 0, 1))
     vectors = noise_ref[...].astype(jnp.bfloat16)
-    for rows, copy in stream(basis_hbm, basis_ref, sems):
+    every = jnp.zeros((nz, basis_ref.shape[0]), f32)
+    for at, copy in started:
         copy.wait()
-        project(vectors, basis_ref, rows, full_ref)
-    q_ref[...] = directions(full_ref, nz)
+        every = every + project(vectors[:, at], basis_ref[:, at])
+    own_layer(every, sums_ref)
+    q_ref[...] = exact_dot(sums_ref[...], group(nz, share, 0))
 
 
 def scan_slabs(sd, nz, got_ref, parts):
@@ -181,7 +194,7 @@
     return carries, energy
 
 
-def owner_kernel(nz, width, layers_ref, got_ref, out_ref, energy_ref):
+def owner_kernel(nz, width, layers_ref, got_ref, q_in, bends_in, out_ref, energy_ref, q_ref, bends_ref):
     blocks = got_ref.shape[0]
     parts = split(width)[0]
     k = layers_ref.shape[0]
@@ -196,11 +209,13 @@
         squares = wide(got_ref, n, k + 1, 1, parts)
         deeper = deeper + carries[n] * (carries[n] * squares - rows)
     energy_ref[...] = jnp.broadcast_to(total(energy) / k, energy_ref.shape)
+    q_ref[...] = q_in[...]
+    bends_ref[...] = bends_in[...]
 
 
 def gradient_kernel(
     depth_count, layers_ref, got_ref, model_ref, rate_ref, w_ref, obs_ref, q_ref, basis_hbm,
-    gradient_ref, out_ref, basis_ref, spread_ref, full_ref, sems
+    gradient_ref, out_ref, basis_ref, sums_ref, sems
 ):
     started = stream(basis_hbm, basis_ref, sems)
     blocks = got_ref.shape[0]
@@ -229,53 +244,54 @@
             deeper = deeper + products[z]
             data = jnp.sum(jnp.where(sd < first + z, deeper, 0.0), axis=0, keepdims=True) + below_sum
             gradient_ref[z : z + 1, lanes] = model[z : z + 1] - coef[z : z + 1] / k * data
-    row = lax.broadcasted_iota(jnp.int32, spread_ref.shape, 0)
-    column = lax.broadcasted_iota(jnp.int32, spread_ref.shape, 1)
-    spread_ref[...] = jnp.where(row == column // nz, 1.0, 0.0).astype(jnp.bfloat16)
     vectors = gradient_ref[...].astype(jnp.bfloat16)
-    for rows, copy in started:
+    every = jnp.zeros((nz, basis_ref.shape[0]), f32)
+    for at, copy in started:
         copy.wait()
-        project(vectors, basis_ref, rows, full_ref)
-    line = directions(full_ref, nz)
-    for n in range(blocks):
-        out_ref[n, 0:1, :] = line
-        out_ref[n, 1:2, :] = q_ref[...]
+        every = every + project(vectors[:, at], basis_ref[:, at])
+    own_layer(every, sums_ref)
+    both = exact_dot(sums_ref[...], group(nz, 0, 0)) + q_ref[...]
+    for n in range(blocks):
+        out_ref[n] = both
 
 
 def proposal_kernel(
-    depth_count, width, layers_ref, got_ref, curvature_ref, gradient_ref, model_ref, rate_ref, w_ref,
-    obs_ref, noise_ref, basis_ref, spread_ref, proposal_ref, out_ref, energy_ref
+    depth_count, width, layers_ref, got_ref, bends_ref, gradient_ref, model_ref, rate_ref, w_ref,
+    obs_ref, noise_ref, basis_ref, proposal_ref, out_ref, energy_ref
 ):
     blocks = out_ref.shape[0]
     parts = split(width)[0]
     nz, columns = model_ref.shape
     k = w_ref.shape[0]
-    rank, total_rows = spread_ref.shape
-    projected = got_ref[0, 0:2, :]
+    projected = got_ref[0]
     for n in range(1, blocks):
-        projected = projected + got_ref[n, 0:2, :]
-    curvature = curvature_ref[...]
+        projected = projected + got_ref[n]
+    p = exact_dot(projected, group(nz, 0, 1))
+    q = exact_dot(projected, group(nz, LANES // nz, 1))
+    curvature = bends_ref[...]
     damping = curvature / (1.0 + curvature)
     shrink = 1.0 - 1.0 / jnp.sqrt(1.0 + curvature)
-    mix = (damping * projected[0:1] - shrink * projected[1:2]).astype(jnp.bfloat16)
-    spread = jnp.dot(jnp.broadcast_to(mix, (nz, rank)), spread_ref[...], preferred_element_type=f32)
-    row = lax.broadcasted_iota(jnp.int32, (nz, total_rows), 0)
-    column = lax.broadcasted_iota(jnp.int32, (nz, total_rows), 1)
-    weights = jnp.where(row == column % nz, spread, 0.0).astype(jnp.bfloat16)
-    correction = jnp.dot(weights, basis_ref[...], preferred_element_type=f32)
-    proposal_ref[...] = model_ref[...] - gradient_ref[...] + noise_ref[...] + correction
-
+    mix = (damping * p - shrink * q).astype(jnp.bfloat16).astype(f32)
+    layer = lax.broadcasted_iota(jnp.int32, (nz, LANES), 0)
+    lane = lax.broadcasted_iota(jnp.int32, (nz, LANES), 1)
+    weights = jnp.concatenate(
+        [jnp.where(layer == lane % nz, mix[i : i + 1, :], 0.0) for i in range(mix.shape[0])], axis=1
+    ).astype(jnp.bfloat16)
     sd = widen(layers_ref, width)
     first = lax.axis_index("depth") * nz
-    energy = jnp.zeros((1, 1), f32)
+    misfit = jnp.zeros(sd.shape, f32)
+    square = jnp.zeros((nz, width), f32)
     for n in range(blocks):
         lanes = slice(n * width, (n + 1) * width)
-        model = proposal_ref[:, lanes]
+        correction = jnp.dot(weights, basis_ref[:, lanes], preferred_element_type=f32)
+        model = model_ref[:, lanes] - gradient_ref[:, lanes] + noise_ref[:, lanes] + correction
+        proposal_ref[:, lanes] = model
         coef = rate_ref[:, lanes] * (1.0 / depth_count) * jnp.exp(0.5 * model)
         rows, through, squares, part = summarize(coef, w_ref[:, lanes], sd, first, obs_ref, lanes)
         write_summary(out_ref, n, rows, through, squares, parts)
-        energy = energy + total(part) / k + 0.5 * total(model * model)
-    energy_ref[...] = jnp.broadcast_to(energy, energy_ref.shape)
+        misfit = misfit + part
+        square = square + model * model
+    energy_ref[...] = jnp.broadcast_to(total(misfit) / k + 0.5 * total(square), energy_ref.shape)
 
 
 def energy_kernel(nz, width, layers_ref, got_ref, first_ref, owner_ref, next_ref, out_ref):
@@ -328,7 +344,7 @@
     def exchange(x):
         return lax.all_to_all(x, "depth", 0, 0)
 
-    sent, energy_first, layers, model, rate, w, obs, noise, bends = call(
+    sent, energy_first, layers, model, rate, w, obs, noise, curved = call(
         functools.partial(first_kernel, depth_count, slabs),
         [summary, scalar, struct((sources, LANES), jnp.int32), field, struct((1, columns), f32),
          struct(wavelets.shape, f32), struct(observed.shape, f32), field, struct((1, rank), f32)],
@@ -339,26 +355,27 @@
     )
     got = exchange(sent)
     flat = basis.reshape(rank * nz, columns)
-    buffers = [pltpu.VMEM((rank * nz, nz), f32), dma((8,))]
-    (q,) = call(
-        functools.partial(noise_kernel, nz), [struct((1, rank), f32)], [flat, noise], hbm=(0,),
+    sums = (rank * nz // LANES, LANES)
+    buffers = [pltpu.VMEM(sums, f32), dma((8,))]
+    q, bends = call(
+        functools.partial(noise_kernel, nz), [struct(sums, f32)] * 2, [flat, noise, curved], hbm=(0,),
         scratch=[pltpu.VMEM(flat.shape, flat.dtype)] + buffers, flops=10**8, limit=24,
     )
-    sent, energy_owner = call(
-        functools.partial(owner_kernel, nz, width), [answer, scalar], [layers, got],
+    sent, energy_owner, q, bends = call(
+        functools.partial(owner_kernel, nz, width), [answer, scalar] + [struct(sums, f32)] * 2,
+        [layers, got, q, bends],
     )
     got = exchange(sent)
-    gradient, sent, near, spread = call(
+    gradient, sent, near = call(
         functools.partial(gradient_kernel, depth_count),
-        [field, struct((slabs, 8, rank), f32), struct(flat.shape, flat.dtype),
-         struct((rank, rank * nz), jnp.bfloat16)],
-        [layers, got, model, rate, w, obs, q, flat], hbm=(7,), scratch=buffers, limit=24,
+        [field, struct((slabs,) + sums, f32), struct(flat.shape, flat.dtype)],
+        [layers, got, model, rate, w, obs, q, flat], hbm=(7,), scratch=buffers,
     )
     got = exchange(sent)
     proposal, sent, energy_next = call(
         functools.partial(proposal_kernel, depth_count, width),
         [field, summary, scalar],
-        [layers, got, bends, gradient, model, rate, w, obs, noise, near, spread], limit=24,
+        [layers, got, bends, gradient, model, rate, w, obs, noise, near],
     )
     got = exchange(sent)
     (sent,) = call(

time: 70.4 us -> 64.7 us (0.919)
  blocking collectives: 45.6 us -> 39 us
  Pallas kernels: 19.7 us -> 14.7 us
  starting transfers between devices: 3.38 us -> 7.32 us
  waiting for transfers between devices: 0.7 us -> 2.68 us
    all_to_all x4, blocking collectives: 45.6 us -> 39 us  [exchange(): return lax.all_to_all(x, 'depth', 0, 0)]
    pallas_call x7, Pallas kernels: 19.7 us -> 14.7 us  [call(): pl.pallas_call(kernel, out_shape=outs, in_specs=[far if i in hbm else vme...]
    all_to_all x1, starting transfers between devices: 3.38 us -> 7.32 us  [exchange(): return lax.all_to_all(x, 'depth', 0, 0)]
    all_to_all x1, waiting for transfers between devices: 0.7 us -> 2.68 us  [exchange(): return lax.all_to_all(x, 'depth', 0, 0)]
  transfers between devices with their start and end apart: 1 -> 1, of which waited for: 1 -> 1; matrix products, arithmetic and copies ran while one was open for 0% -> 0% of each run, Pallas kernels for 10% -> 8%
where the time goes in v3:
time: 64.7 us; the launch traced here: 64.3 us
  blocking collectives  39 us (60%)
  Pallas kernels  14.7 us (23%)
  starting transfers between devices  7.32 us (11%)
  waiting for transfers between devices  2.68 us (4%)
  between operations  0.66 us (1%)
    all_to_all x4, blocking collectives, exchange(): return lax.all_to_all(x, 'depth', 0, 0)  39 us
    pallas_call x7, Pallas kernels, call(): pl.pallas_call(kernel, out_shape=outs, in_specs=[far if i in hbm else vme...  14.7 us
    all_to_all x1, starting transfers between devices, exchange(): return lax.all_to_all(x, 'depth', 0, 0)  7.32 us
    all_to_all x1, waiting for transfers between devices, exchange(): return lax.all_to_all(x, 'depth', 0, 0)  2.68 us
  transfers between devices with their start and end apart: 1, of which 1 were waited for; matrix products, arithmetic and copies ran while one was open for 0% of the time, Pallas kernels for 8%

profile of v3, /device:TPU:0, one launch (start us, length us, event | category | flops | bytes accessed | tf_op | source)
XLA Modules:
  0.0 64.3 jit_solution(10051879288722346677)
XLA Ops:
  0.6 2.6 %shard_map.95 = (f32[8,40,128]{2,1,0:T(8,128)}, f32[8,128]{1,0:T(8,128)S(1)}, s32[16,128]{1,0:T(8,128)S(1)}, f32[8,2048]{1,0:T(8,128)S(1)}, f32[1,2048]{1,0:T(1,...) custom-call(s32[16]{0:T(128)} %sd_hbm.1, ...), custom_call_target="tpu_custom_call" | custom-call | flops 1000000 | bytes 1000000 | tf_op jit(solution)/shard_map/pallas_call | solution.py:318
  3.2 7.3 %all-to-all-start = ((f32[8,40,128]{2,1,0:T(8,128)}), f32[8,40,128]{2,1,0:T(8,128)S(1)}, u32[]{:S(2)}, u32[]{:S(2)}) async-start(f32[8,40,128]{2,1,0:T(8,128)} %get-tuple-element.24), calls=%async_computation | async-start | bytes 327680 | tf_op jit(solution)/shard_map/all_to_all | solution.py:345
  10.6 4.9 %shard_map.96 = (f32[16,128]{1,0:T(8,128)S(1)}, f32[16,128]{1,0:T(8,128)S(1)}) custom-call(bf16[2048,2048]{1,0:T(8,128)(2,1)} %bitcast.4, f32[8,2048]{1,0:T(8,128)S(1)} %get-tuple-element.25.noise_ref, f32[1,256]{1,0:T(1,128)S(1)} %get-tuple-element.26.curvature_ref), custom_call_target="tpu_custom_call" | custom-call | flops 100000000 | bytes 100000000 | tf_op jit(solution)/shard_map/pallas_call | solution.py:318
  15.4 2.7 %all-to-all-done.got_ref = f32[8,40,128]{2,1,0:T(8,128)S(1)} async-done(((f32[8,40,128]{2,1,0:T(8,128)}), f32[8,40,128]{2,1,0:T(8,128)S(1)}, u32[]{:S(2)}, u32[]{:S(2)}) %all-to-all-start) | async-done | bytes 163872 | tf_op jit(solution)/shard_map/all_to_all | solution.py:345
  18.1 0.1 shard_map.97
  18.3 10.7 %all_to_all.25.got_ref = f32[8,40,128]{2,1,0:T(8,128)S(1)} all-to-all(f32[8,40,128]{2,1,0:T(8,128)S(1)} %get-tuple-element.29), channel_id=1, replica_groups=mesh['chain'=4,'depth'=8] {'depth'}, dimensions={0} | all-to-all | bytes 327680 | tf_op jit(solution)/shard_map/all_to_all | solution.py:345
  28.9 4.2 %shard_map.98 = (f32[8,2048]{1,0:T(8,128)S(1)}, f32[8,16,128]{2,1,0:T(8,128)S(1)}, bf16[2048,2048]{1,0:T(8,128)(2,1)S(1)}) custom-call(s32[16,128]{1,0:T(8,128)S(1)} %get-tuple-element.23.layers_ref, f32[8,40,128]{2,1,0:T(8,128)S(1)} %all_to_all.25.got_ref, f32[8,2048]{1,0:T(8,128)S(1)} %get-tuple-element.30.model_ref, ...), custom_call_target="tpu_custom_call" | custom-call | flops 1000000 | bytes 1000000 | tf_op jit(solution)/shard_map/pallas_call | solution.py:318
  33.2 9.3 %all_to_all.26.got_ref = f32[8,16,128]{2,1,0:T(8,128)S(1)} all-to-all(f32[8,16,128]{2,1,0:T(8,128)S(1)} %get-tuple-element.35), channel_id=1, replica_groups=mesh['chain'=4,'depth'=8] {'depth'}, dimensions={0} | all-to-all | bytes 131072 | tf_op jit(solution)/shard_map/all_to_all | solution.py:345
  42.5 2.2 %shard_map.99 = (f32[8,2048]{1,0:T(8,128)}, f32[8,40,128]{2,1,0:T(8,128)S(1)}, f32[8,128]{1,0:T(8,128)S(1)}) custom-call(s32[16,128]{1,0:T(8,128)S(1)} %get-tuple-element.23.layers_ref, f32[8,16,128]{2,1,0:T(8,128)S(1)} %all_to_all.26.got_ref, f32[16,128]{1,0:T(8,128)S(1)} %get-tuple-element.36.bends_ref, f32[8,2048]{1,0:T(8,128)S(1)} %get-tuple-element.37.gradient_ref, ...), custom_call_target="tpu_custom_call" | custom-call | flops 1000000 | bytes 1000000 | tf_op jit(solution)/shard_map/pallas_call | solution.py:318
  44.7 9.9 %all_to_all.27.got_ref = f32[8,40,128]{2,1,0:T(8,128)S(1)} all-to-all(f32[8,40,128]{2,1,0:T(8,128)S(1)} %get-tuple-element.40), channel_id=1, replica_groups=mesh['chain'=4,'depth'=8] {'depth'}, dimensions={0} | all-to-all | bytes 327680 | tf_op jit(solution)/shard_map/all_to_all | solution.py:345
  54.6 0.1 shard_map.100
  54.7 9.0 %all_to_all.28.got_ref = f32[8,8,128]{2,1,0:T(8,128)S(1)} all-to-all(f32[8,8,128]{2,1,0:T(8,128)S(1)} %shard_map.100), channel_id=1, replica_groups=mesh['chain'=4,'depth'=8] {'depth'}, dimensions={0} | all-to-all | bytes 65536 | tf_op jit(solution)/shard_map/all_to_all | solution.py:345
  63.8 0.5 shard_map.101
Async XLA Ops:
  3.2 14.9 %all-to-all-start = ((f32[8,40,128]{2,1,0:T(8,128)}), f32[8,40,128]{2,1,0:T(8,128)S(1)}, u32[]{:S(2)}, u32[]{:S(2)}) async-start(f32[8,40,128]{2,1,0:T(8,128)} %get-tuple-element.24), calls=%async_computation | async-start | bytes 327680 | tf_op jit(solution)/shard_map/all_to_all | solution.py:345

commit v4 on v3

--- a/solution.py
+++ b/solution.py
@@ -77,10 +77,21 @@
     put_wide(out_ref, n, k + 1, squares, parts)
 
 
+def expand(row, nz):
+    rank, share = row.shape[1], LANES // nz
+    line = lax.broadcasted_iota(jnp.int32, (rank // share, rank), 0)
+    entry = lax.broadcasted_iota(jnp.int32, (rank // share, rank), 1)
+    mine = jnp.where(entry // share == line, jnp.broadcast_to(row, line.shape), 0.0)
+    entry = lax.broadcasted_iota(jnp.int32, (rank, LANES), 0)
+    lane = lax.broadcasted_iota(jnp.int32, (rank, LANES), 1)
+    pick = jnp.where(entry % share == lane // nz, 1.0, 0.0)
+    return jnp.dot(mine, pick, precision=lax.Precision.HIGHEST, preferred_element_type=f32)
+
+
 def first_kernel(
     depth_count, blocks, sd_hbm, model_hbm, rate_hbm, w_hbm, obs_hbm, noise_hbm, curvature_hbm,
-    out_ref, energy_ref, layers_ref, model_ref, rate_ref, w_ref, obs_ref, noise_ref, curvature_ref,
-    sd_ref, sems, obs_sems
+    out_ref, energy_ref, layers_ref, model_ref, rate_ref, w_ref, obs_ref, noise_ref, bends_ref,
+    curvature_ref, sd_ref, sems, obs_sems
 ):
     nz, columns = model_ref.shape
     k = w_ref.shape[0]
@@ -89,8 +100,8 @@
     copies = [
         pltpu.make_async_copy(src, dst, sems.at[i])
         for i, (src, dst) in enumerate([
-            (sd_hbm, sd_ref), (model_hbm, model_ref), (rate_hbm, rate_ref), (w_hbm, w_ref),
-            (noise_hbm, noise_ref), (curvature_hbm, curvature_ref),
+            (curvature_hbm, curvature_ref), (sd_hbm, sd_ref), (model_hbm, model_ref), (rate_hbm, rate_ref),
+            (w_hbm, w_ref), (noise_hbm, noise_ref),
         ])
     ]
     pieces = obs_sems.shape[0]
@@ -99,13 +110,14 @@
     for i in range(pieces):
         at = pl.ds(i * piece, piece)
         obs_copies.append(pltpu.make_async_copy(obs_hbm.at[:, :, at], obs_ref.at[:, :, at], obs_sems.at[i]))
-    for copy in copies[:4]:
+    for copy in copies[:5]:
         copy.start()
     for copy in obs_copies:
         copy.start()
-    for copy in copies[4:]:
-        copy.start()
-    for copy in copies[:4]:
+    copies[5].start()
+    copies[0].wait()
+    bends_ref[...] = expand(curvature_ref[...], nz)
+    for copy in copies[1:5]:
         copy.wait()
     layers_ref[...] = source_layers(sd_ref, k)
     sd = widen(layers_ref, width)
@@ -123,18 +135,25 @@
         misfit = misfit + part
         square = square + model * model
     energy_ref[...] = jnp.broadcast_to(total(misfit) / k + 0.5 * total(square), energy_ref.shape)
-    for copy in copies[4:]:
-        copy.wait()
-
-
-def group(nz, offset, expand):
-    one = lax.broadcasted_iota(jnp.int32, (LANES, LANES), 1 - expand)
-    each = lax.broadcasted_iota(jnp.int32, (LANES, LANES), expand)
-    return jnp.where(one == each // nz + offset, 1.0, 0.0)
-
-
-def exact_dot(a, b):
-    return jnp.dot(a, b, precision=lax.Precision.HIGHEST, preferred_element_type=f32)
+    copies[5].wait()
+
+
+def group_sums(x, nz):
+    step = 1
+    while step < nz:
+        x = x + pltpu.roll(x, step, 1)
+        step *= 2
+    return x
+
+
+def spread(x, nz):
+    lane = lax.broadcasted_iota(jnp.int32, x.shape, 1)
+    x = jnp.where(lane % nz == nz - 1, x, 0.0)
+    step = 1
+    while step < nz:
+        x = x + pltpu.roll(x, LANES - step, 1)
+        step *= 2
+    return x
 
 
 def project(vectors, basis_ref):
@@ -142,12 +161,16 @@
 
 
 def own_layer(every, sums_ref):
-    nz = every.shape[0]
+    nz = every.shape[0] // 2
+    tiles = every.shape[1] // LANES
     layer = lax.broadcasted_iota(jnp.int32, (nz, LANES), 0)
     lane = lax.broadcasted_iota(jnp.int32, (nz, LANES), 1)
-    for t in range(every.shape[1] // LANES):
-        mine = jnp.where(layer == lane % nz, every[:, t * LANES : (t + 1) * LANES], 0.0)
-        sums_ref[t : t + 1, :] = jnp.sum(mine, axis=0, keepdims=True)
+    own = layer == lane % nz
+    for which in range(2):
+        for t in range(tiles):
+            mine = jnp.where(own, every[which * nz : (which + 1) * nz, t * LANES : (t + 1) * LANES], 0.0)
+            at = which * tiles + t
+            sums_ref[at : at + 1, :] = jnp.sum(mine, axis=0, keepdims=True)
 
 
 def stream(basis_hbm, basis_ref, sems):
@@ -162,22 +185,6 @@
     return started
 
 
-def noise_kernel(nz, basis_hbm, noise_ref, curvature_ref, q_ref, bends_ref, basis_ref, sums_ref, sems):
-    started = stream(basis_hbm, basis_ref, sems)
-    share = LANES // nz
-    sums_ref[...] = jnp.zeros_like(sums_ref)
-    for i in range(sums_ref.shape[0]):
-        sums_ref[i : i + 1, 0:share] = curvature_ref[:, i * share : (i + 1) * share]
-    bends_ref[...] = exact_dot(sums_ref[...], group(nz, 0, 1))
-    vectors = noise_ref[...].astype(jnp.bfloat16)
-    every = jnp.zeros((nz, basis_ref.shape[0]), f32)
-    for at, copy in started:
-        copy.wait()
-        every = every + project(vectors[:, at], basis_ref[:, at])
-    own_layer(every, sums_ref)
-    q_ref[...] = exact_dot(sums_ref[...], group(nz, share, 0))
-
-
 def scan_slabs(sd, nz, got_ref, parts):
     blocks = got_ref.shape[0]
     k = sd.shape[0]
@@ -194,7 +201,7 @@
     return carries, energy
 
 
-def owner_kernel(nz, width, layers_ref, got_ref, q_in, bends_in, out_ref, energy_ref, q_ref, bends_ref):
+def owner_kernel(nz, width, layers_ref, got_ref, out_ref, energy_ref):
     blocks = got_ref.shape[0]
     parts = split(width)[0]
     k = layers_ref.shape[0]
@@ -209,12 +216,10 @@
         squares = wide(got_ref, n, k + 1, 1, parts)
         deeper = deeper + carries[n] * (carries[n] * squares - rows)
     energy_ref[...] = jnp.broadcast_to(total(energy) / k, energy_ref.shape)
-    q_ref[...] = q_in[...]
-    bends_ref[...] = bends_in[...]
 
 
 def gradient_kernel(
-    depth_count, layers_ref, got_ref, model_ref, rate_ref, w_ref, obs_ref, q_ref, basis_hbm,
+    depth_count, layers_ref, got_ref, model_ref, rate_ref, w_ref, obs_ref, noise_ref, basis_hbm,
     gradient_ref, out_ref, basis_ref, sums_ref, sems
 ):
     started = stream(basis_hbm, basis_ref, sems)
@@ -244,13 +249,17 @@
             deeper = deeper + products[z]
             data = jnp.sum(jnp.where(sd < first + z, deeper, 0.0), axis=0, keepdims=True) + below_sum
             gradient_ref[z : z + 1, lanes] = model[z : z + 1] - coef[z : z + 1] / k * data
-    vectors = gradient_ref[...].astype(jnp.bfloat16)
-    every = jnp.zeros((nz, basis_ref.shape[0]), f32)
+    tiles = sums_ref.shape[0] // 2
+    vectors = jnp.concatenate([gradient_ref[...], noise_ref[...]], axis=0).astype(jnp.bfloat16)
+    every = jnp.zeros((2 * nz, basis_ref.shape[0]), f32)
     for at, copy in started:
         copy.wait()
         every = every + project(vectors[:, at], basis_ref[:, at])
     own_layer(every, sums_ref)
-    both = exact_dot(sums_ref[...], group(nz, 0, 0)) + q_ref[...]
+    p = group_sums(sums_ref[0:tiles, :], nz)
+    q = group_sums(sums_ref[tiles : 2 * tiles, :], nz)
+    lane = lax.broadcasted_iota(jnp.int32, p.shape, 1)
+    both = jnp.where(lane % nz == nz - 1, p, pltpu.roll(q, LANES - nz // 2, 1))
     for n in range(blocks):
         out_ref[n] = both
 
@@ -266,8 +275,8 @@
     projected = got_ref[0]
     for n in range(1, blocks):
         projected = projected + got_ref[n]
-    p = exact_dot(projected, group(nz, 0, 1))
-    q = exact_dot(projected, group(nz, LANES // nz, 1))
+    p = spread(projected, nz)
+    q = spread(pltpu.roll(projected, nz // 2, 1), nz)
     curvature = bends_ref[...]
     damping = curvature / (1.0 + curvature)
     shrink = 1.0 - 1.0 / jnp.sqrt(1.0 + curvature)
@@ -340,36 +349,31 @@
     scalar = struct((8, LANES), f32)
     field = struct((nz, columns), f32)
     dma = pltpu.SemaphoreType.DMA
+    flat = basis.reshape(rank * nz, columns)
+    sums = (rank * nz // LANES, LANES)
 
     def exchange(x):
         return lax.all_to_all(x, "depth", 0, 0)
 
-    sent, energy_first, layers, model, rate, w, obs, noise, curved = call(
+    sent, energy_first, layers, model, rate, w, obs, noise, bends = call(
         functools.partial(first_kernel, depth_count, slabs),
         [summary, scalar, struct((sources, LANES), jnp.int32), field, struct((1, columns), f32),
-         struct(wavelets.shape, f32), struct(observed.shape, f32), field, struct((1, rank), f32)],
+         struct(wavelets.shape, f32), struct(observed.shape, f32), field, struct(sums, f32)],
         [source_depth, model_field, column_rate.reshape(1, columns), wavelets, observed, noise_draw,
          curvature.reshape(1, rank)],
         hbm=range(7),
-        scratch=[pltpu.SMEM((sources,), jnp.int32), dma((6,)), dma((8,))],
+        scratch=[pltpu.VMEM((1, rank), f32), pltpu.SMEM((sources,), jnp.int32), dma((6,)), dma((8,))],
     )
     got = exchange(sent)
-    flat = basis.reshape(rank * nz, columns)
-    sums = (rank * nz // LANES, LANES)
-    buffers = [pltpu.VMEM(sums, f32), dma((8,))]
-    q, bends = call(
-        functools.partial(noise_kernel, nz), [struct(sums, f32)] * 2, [flat, noise, curved], hbm=(0,),
-        scratch=[pltpu.VMEM(flat.shape, flat.dtype)] + buffers, flops=10**8, limit=24,
-    )
-    sent, energy_owner, q, bends = call(
-        functools.partial(owner_kernel, nz, width), [answer, scalar] + [struct(sums, f32)] * 2,
-        [layers, got, q, bends],
+    sent, energy_owner = call(
+        functools.partial(owner_kernel, nz, width), [answer, scalar], [layers, got],
     )
     got = exchange(sent)
     gradient, sent, near = call(
         functools.partial(gradient_kernel, depth_count),
         [field, struct((slabs,) + sums, f32), struct(flat.shape, flat.dtype)],
-        [layers, got, model, rate, w, obs, q, flat], hbm=(7,), scratch=buffers,
+        [layers, got, model, rate, w, obs, noise, flat], hbm=(7,),
+        scratch=[pltpu.VMEM((2 * sums[0], LANES), f32), dma((8,))],
     )
     got = exchange(sent)
     proposal, sent, energy_next = call(

time: 64.7 us -> 63.3 us (0.978)
  blocking collectives: 39 us -> 53.1 us
  starting transfers between devices: 7.32 us -> 0 us
  Pallas kernels: 14.7 us -> 9.2 us
  waiting for transfers between devices: 2.68 us -> 0 us
    all_to_all x4 -> x5, blocking collectives: 39 us -> 53.1 us  [exchange(): return lax.all_to_all(x, 'depth', 0, 0)]
    all_to_all x1 -> x0, starting transfers between devices: 7.32 us -> none  [exchange(): return lax.all_to_all(x, 'depth', 0, 0)]
    pallas_call x7 -> x6, Pallas kernels: 14.7 us -> 9.2 us  [call(): pl.pallas_call(kernel, out_shape=outs, in_specs=[far if i in hbm else vme...]
    all_to_all x1 -> x0, waiting for transfers between devices: 2.68 us -> none  [exchange(): return lax.all_to_all(x, 'depth', 0, 0)]
  transfers between devices with their start and end apart: 1 -> 0, of which waited for: 1 -> 0; matrix products, arithmetic and copies ran while one was open for 0% -> 0% of each run, Pallas kernels for 8% -> 0%
where the time goes in v4:
time: 63.3 us; the launch traced here: 63 us
  blocking collectives  53.1 us (84%)
  Pallas kernels  9.2 us (15%)
  between operations  0.65 us (1%)
    all_to_all x5, blocking collectives, exchange(): return lax.all_to_all(x, 'depth', 0, 0)  53.1 us
    pallas_call x6, Pallas kernels, call(): pl.pallas_call(kernel, out_shape=outs, in_specs=[far if i in hbm else vme...  9.2 us

profile of v4, /device:TPU:0, one launch (start us, length us, event | category | flops | bytes accessed | tf_op | source)
XLA Modules:
  0.0 63.0 jit_solution(4178098300612771348)
XLA Ops:
  0.6 1.9 %shard_map.95 = (f32[8,40,128]{2,1,0:T(8,128)S(1)}, f32[8,128]{1,0:T(8,128)S(1)}, s32[16,128]{1,0:T(8,128)S(1)}, f32[8,2048]{1,0:T(8,128)S(1)}, f32[1,2048]{1,0:...) custom-call(s32[16]{0:T(128)} %sd_hbm.1, ...), custom_call_target="tpu_custom_call" | custom-call | flops 1000000 | bytes 1000000 | tf_op jit(solution)/shard_map/pallas_call | solution.py:327
  2.6 14.7 %all_to_all.25.got_ref = f32[8,40,128]{2,1,0:T(8,128)S(1)} all-to-all(f32[8,40,128]{2,1,0:T(8,128)S(1)} %get-tuple-element.20), channel_id=1, replica_groups=mesh['chain'=4,'depth'=8] {'depth'}, dimensions={0} | all-to-all | bytes 327680 | tf_op jit(solution)/shard_map/all_to_all | solution.py:356
  17.2 0.2 shard_map.96
  17.4 10.2 %all_to_all.26.got_ref = f32[8,40,128]{2,1,0:T(8,128)S(1)} all-to-all(f32[8,40,128]{2,1,0:T(8,128)S(1)} %get-tuple-element.21), channel_id=1, replica_groups=mesh['chain'=4,'depth'=8] {'depth'}, dimensions={0} | all-to-all | bytes 327680 | tf_op jit(solution)/shard_map/all_to_all | solution.py:356
  27.6 4.3 %shard_map.97 = (f32[8,2048]{1,0:T(8,128)S(1)}, f32[8,16,128]{2,1,0:T(8,128)S(1)}, bf16[2048,2048]{1,0:T(8,128)(2,1)S(1)}) custom-call(s32[16,128]{1,0:T(8,128)S(1)} %get-tuple-element.19.layers_ref, f32[8,40,128]{2,1,0:T(8,128)S(1)} %all_to_all.26.got_ref, f32[8,2048]{1,0:T(8,128)S(1)} %get-tuple-element.22.model_ref, ...), custom_call_target="tpu_custom_call" | custom-call | flops 1000000 | bytes 1000000 | tf_op jit(solution)/shard_map/pallas_call | solution.py:327
  31.8 9.3 %all_to_all.27.got_ref = f32[8,16,128]{2,1,0:T(8,128)S(1)} all-to-all(f32[8,16,128]{2,1,0:T(8,128)S(1)} %get-tuple-element.27), channel_id=1, replica_groups=mesh['chain'=4,'depth'=8] {'depth'}, dimensions={0} | all-to-all | bytes 131072 | tf_op jit(solution)/shard_map/all_to_all | solution.py:356
  41.1 2.2 %shard_map.98 = (f32[8,2048]{1,0:T(8,128)}, f32[8,40,128]{2,1,0:T(8,128)S(1)}, f32[8,128]{1,0:T(8,128)S(1)}) custom-call(s32[16,128]{1,0:T(8,128)S(1)} %get-tuple-element.19.layers_ref, f32[8,16,128]{2,1,0:T(8,128)S(1)} %all_to_all.27.got_ref, f32[16,128]{1,0:T(8,128)S(1)} %get-tuple-element.28.bends_ref, f32[8,2048]{1,0:T(8,128)S(1)} %get-tuple-element.29.gradient_ref, ...), custom_call_target="tpu_custom_call" | custom-call | flops 1000000 | bytes 1000000 | tf_op jit(solution)/shard_map/pallas_call | solution.py:327
  43.4 9.9 %all_to_all.28.got_ref = f32[8,40,128]{2,1,0:T(8,128)S(1)} all-to-all(f32[8,40,128]{2,1,0:T(8,128)S(1)} %get-tuple-element.32), channel_id=1, replica_groups=mesh['chain'=4,'depth'=8] {'depth'}, dimensions={0} | all-to-all | bytes 327680 | tf_op jit(solution)/shard_map/all_to_all | solution.py:356
  53.3 0.1 shard_map.99
  53.4 9.0 %all_to_all.29.got_ref = f32[8,8,128]{2,1,0:T(8,128)S(1)} all-to-all(f32[8,8,128]{2,1,0:T(8,128)S(1)} %shard_map.99), channel_id=1, replica_groups=mesh['chain'=4,'depth'=8] {'depth'}, dimensions={0} | all-to-all | bytes 65536 | tf_op jit(solution)/shard_map/all_to_all | solution.py:356
  62.5 0.5 shard_map.100

commit v5 on v4

--- a/solution.py
+++ b/solution.py
@@ -219,10 +219,9 @@
 
 
 def gradient_kernel(
-    depth_count, layers_ref, got_ref, model_ref, rate_ref, w_ref, obs_ref, noise_ref, basis_hbm,
-    gradient_ref, out_ref, basis_ref, sums_ref, sems
+    depth_count, layers_ref, got_ref, model_ref, rate_ref, w_ref, obs_ref, noise_ref, basis_ref,
+    gradient_ref, out_ref, sums_ref
 ):
-    started = stream(basis_hbm, basis_ref, sems)
     blocks = got_ref.shape[0]
     nz, columns = model_ref.shape
     width = columns // blocks
@@ -231,8 +230,18 @@
     sd = widen(layers_ref, width)
     first = lax.axis_index("depth") * nz
     above = sd < first
+    tiles = sums_ref.shape[0] // 2
+    piece = max(width, min(columns, 2 * LANES))
+    every = jnp.zeros((2 * nz, basis_ref.shape[0]), f32)
+
+    def add_projection(every, at):
+        vectors = jnp.concatenate([gradient_ref[:, at], noise_ref[:, at]], axis=0).astype(jnp.bfloat16)
+        return every + project(vectors, basis_ref[:, at])
+
     for n in range(blocks):
         lanes = slice(n * width, (n + 1) * width)
+        if n > 0 and lanes.start % piece == 0:
+            every = add_projection(every, slice(lanes.start - piece, lanes.start))
         model = model_ref[:, lanes]
         coef = rate_ref[:, lanes] * (1.0 / depth_count) * jnp.exp(0.5 * model)
         decay = jnp.exp(-coef)
@@ -249,12 +258,7 @@
             deeper = deeper + products[z]
             data = jnp.sum(jnp.where(sd < first + z, deeper, 0.0), axis=0, keepdims=True) + below_sum
             gradient_ref[z : z + 1, lanes] = model[z : z + 1] - coef[z : z + 1] / k * data
-    tiles = sums_ref.shape[0] // 2
-    vectors = jnp.concatenate([gradient_ref[...], noise_ref[...]], axis=0).astype(jnp.bfloat16)
-    every = jnp.zeros((2 * nz, basis_ref.shape[0]), f32)
-    for at, copy in started:
-        copy.wait()
-        every = every + project(vectors[:, at], basis_ref[:, at])
+    every = add_projection(every, slice(columns - piece, columns))
     own_layer(every, sums_ref)
     p = group_sums(sums_ref[0:tiles, :], nz)
     q = group_sums(sums_ref[tiles : 2 * tiles, :], nz)
@@ -286,13 +290,20 @@
     weights = jnp.concatenate(
         [jnp.where(layer == lane % nz, mix[i : i + 1, :], 0.0) for i in range(mix.shape[0])], axis=1
     ).astype(jnp.bfloat16)
+
+    def correct(n):
+        return jnp.dot(weights, basis_ref[:, n * width : (n + 1) * width], preferred_element_type=f32)
+
+    corrections = [correct(0)]
     sd = widen(layers_ref, width)
     first = lax.axis_index("depth") * nz
     misfit = jnp.zeros(sd.shape, f32)
     square = jnp.zeros((nz, width), f32)
     for n in range(blocks):
         lanes = slice(n * width, (n + 1) * width)
-        correction = jnp.dot(weights, basis_ref[:, lanes], preferred_element_type=f32)
+        correction = corrections.pop()
+        if n + 1 < blocks:
+            corrections.append(correct(n + 1))
         model = model_ref[:, lanes] - gradient_ref[:, lanes] + noise_ref[:, lanes] + correction
         proposal_ref[:, lanes] = model
         coef = rate_ref[:, lanes] * (1.0 / depth_count) * jnp.exp(0.5 * model)
@@ -366,20 +377,20 @@
     )
     got = exchange(sent)
     sent, energy_owner = call(
-        functools.partial(owner_kernel, nz, width), [answer, scalar], [layers, got],
+        functools.partial(owner_kernel, nz, width), [answer, scalar], [layers, got], flops=10**10,
     )
     got = exchange(sent)
-    gradient, sent, near = call(
+    gradient, sent = call(
         functools.partial(gradient_kernel, depth_count),
-        [field, struct((slabs,) + sums, f32), struct(flat.shape, flat.dtype)],
-        [layers, got, model, rate, w, obs, noise, flat], hbm=(7,),
-        scratch=[pltpu.VMEM((2 * sums[0], LANES), f32), dma((8,))],
+        [field, struct((slabs,) + sums, f32)],
+        [layers, got, model, rate, w, obs, noise, flat],
+        scratch=[pltpu.VMEM((2 * sums[0], LANES), f32)],
     )
     got = exchange(sent)
     proposal, sent, energy_next = call(
         functools.partial(proposal_kernel, depth_count, width),
         [field, summary, scalar],
-        [layers, got, bends, gradient, model, rate, w, obs, noise, near],
+        [layers, got, bends, gradient, model, rate, w, obs, noise, flat],
     )
     got = exchange(sent)
     (sent,) = call(

time: 63.3 us -> 62.1 us (0.981)
  Pallas kernels: 9.2 us -> 7.76 us
    pallas_call x6, Pallas kernels: 9.2 us -> 7.76 us  [call(): pl.pallas_call(kernel, out_shape=outs, in_specs=[far if i in hbm else vme...]
where the time goes in v5:
time: 62.1 us; the launch traced here: 61.8 us
  blocking collectives  53.4 us (86%)
  Pallas kernels  7.76 us (12%)
  between operations  0.66 us (1%)
    all_to_all x5, blocking collectives, exchange(): return lax.all_to_all(x, 'depth', 0, 0)  53.4 us
    pallas_call x6, Pallas kernels, call(): pl.pallas_call(kernel, out_shape=outs, in_specs=[far if i in hbm else vme...  7.76 us

profile of v5, /device:TPU:0, one launch (start us, length us, event | category | flops | bytes accessed | tf_op | source)
XLA Modules:
  0.0 61.8 jit_solution(4967277044601504651)
XLA Ops:
  0.6 0.0 slice-start
  0.6 2.0 %shard_map.95 = (f32[8,40,128]{2,1,0:T(8,128)S(1)}, f32[8,128]{1,0:T(8,128)S(1)}, s32[16,128]{1,0:T(8,128)S(1)}, f32[8,2048]{1,0:T(8,128)S(1)}, f32[1,2048]{1,0:...) custom-call(s32[16]{0:T(128)} %sd_hbm.1, ...), custom_call_target="tpu_custom_call" | custom-call | flops 1000000 | bytes 1000000 | tf_op jit(solution)/shard_map/pallas_call | solution.py:338
  2.7 14.7 %all_to_all.25.got_ref = f32[8,40,128]{2,1,0:T(8,128)S(1)} all-to-all(f32[8,40,128]{2,1,0:T(8,128)S(1)} %get-tuple-element.19), channel_id=1, replica_groups=mesh['chain'=4,'depth'=8] {'depth'}, dimensions={0} | all-to-all | bytes 327680 | tf_op jit(solution)/shard_map/all_to_all | solution.py:367
  17.4 0.0 slice-start.1
  17.4 0.1 shard_map.96
  17.5 10.4 %all_to_all.26.got_ref = f32[8,40,128]{2,1,0:T(8,128)S(1)} all-to-all(f32[8,40,128]{2,1,0:T(8,128)S(1)} %get-tuple-element.20), channel_id=1, replica_groups=mesh['chain'=4,'depth'=8] {'depth'}, dimensions={0} | all-to-all | bytes 327680 | tf_op jit(solution)/shard_map/all_to_all | solution.py:367
  28.0 0.0 slice-done
  28.0 0.0 slice-done.1
  28.0 2.7 %shard_map.97 = (f32[8,2048]{1,0:T(8,128)S(1)}, f32[8,16,128]{2,1,0:T(8,128)S(1)}) custom-call(s32[16,128]{1,0:T(8,128)S(1)} %get-tuple-element.18.layers_ref, f32[8,40,128]{2,1,0:T(8,128)S(1)} %all_to_all.26.got_ref, f32[8,2048]{1,0:T(8,128)S(1)} %get-tuple-element.21.model_ref, f32[1,2048]{1,0:T(1,128)S(1)} %get-tuple-element.22.rate_ref, ...), custom_call_target="tpu_custom_call" | custom-call | flops 1000000 | bytes 1000000 | tf_op jit(solution)/shard_map/pallas_call | solution.py:338
  30.7 9.3 %all_to_all.27.got_ref = f32[8,16,128]{2,1,0:T(8,128)S(1)} all-to-all(f32[8,16,128]{2,1,0:T(8,128)S(1)} %get-tuple-element.26), channel_id=1, replica_groups=mesh['chain'=4,'depth'=8] {'depth'}, dimensions={0} | all-to-all | bytes 131072 | tf_op jit(solution)/shard_map/all_to_all | solution.py:367
  40.0 2.2 %shard_map.98 = (f32[8,2048]{1,0:T(8,128)}, f32[8,40,128]{2,1,0:T(8,128)S(1)}, f32[8,128]{1,0:T(8,128)S(1)}) custom-call(s32[16,128]{1,0:T(8,128)S(1)} %get-tuple-element.18.layers_ref, f32[8,16,128]{2,1,0:T(8,128)S(1)} %all_to_all.27.got_ref, f32[16,128]{1,0:T(8,128)S(1)} %get-tuple-element.27.bends_ref, f32[8,2048]{1,0:T(8,128)S(1)} %get-tuple-element.28.gradient_ref, ...), custom_call_target="tpu_custom_call" | custom-call | flops 1000000 | bytes 1000000 | tf_op jit(solution)/shard_map/pallas_call | solution.py:338
  42.2 9.9 %all_to_all.28.got_ref = f32[8,40,128]{2,1,0:T(8,128)S(1)} all-to-all(f32[8,40,128]{2,1,0:T(8,128)S(1)} %get-tuple-element.30), channel_id=1, replica_groups=mesh['chain'=4,'depth'=8] {'depth'}, dimensions={0} | all-to-all | bytes 327680 | tf_op jit(solution)/shard_map/all_to_all | solution.py:367
  52.1 0.1 shard_map.99
  52.3 9.0 %all_to_all.29.got_ref = f32[8,8,128]{2,1,0:T(8,128)S(1)} all-to-all(f32[8,8,128]{2,1,0:T(8,128)S(1)} %shard_map.99), channel_id=1, replica_groups=mesh['chain'=4,'depth'=8] {'depth'}, dimensions={0} | all-to-all | bytes 65536 | tf_op jit(solution)/shard_map/all_to_all | solution.py:367
  61.3 0.5 shard_map.100
  (1 shorter events, 0.0 us)
Async XLA Ops:
  0.6 27.3 %slice-start = ((s8[8388608]{0:T(1024)(128)(4,1)}), s8[4194304]{0:T(1024)(128)(4,1)S(1)}, s32[]{:S(2)}) async-start(s8[8388608]{0:T(1024)(128)(4,1)} %bitcast.4), calls=%async_computation.5 | async-start | bytes 8388608
  17.4 10.6 %slice-start.1 = ((s8[8388608]{0:T(1024)(128)(4,1)}), s8[4194304]{0:T(1024)(128)(4,1)S(1)}, s32[]{:S(2)}) async-start(s8[8388608]{0:T(1024)(128)(4,1)} %bitcast.4), calls=%async_computation.6 | async-start | bytes 8388608

commit v6 on v5

--- a/solution.py
+++ b/solution.py
@@ -321,14 +321,15 @@
     _, energy = scan_slabs(sd, nz, got_ref, split(width)[0])
     drop = first_ref[...] + owner_ref[...] - next_ref[...] - total(energy) / k
     for n in range(blocks):
-        out_ref[n] = drop
-
-
-def final_kernel(cells, got_ref, out_ref):
+        out_ref[n] = drop[0:1, :]
+
+
+def final_kernel(cells, got_ref, proposal_in, out_ref, proposal_ref):
+    proposal_ref[...] = proposal_in[...]
     drop = got_ref[0]
     for n in range(1, got_ref.shape[0]):
         drop = drop + got_ref[n]
-    out_ref[...] = drop[0:1, 0:1] / cells
+    out_ref[...] = drop[:, 0:1] / cells
 
 
 def call(kernel, outs, args, hbm=(), scratch=(), flops=10**6, limit=16):
@@ -373,11 +374,11 @@
         [source_depth, model_field, column_rate.reshape(1, columns), wavelets, observed, noise_draw,
          curvature.reshape(1, rank)],
         hbm=range(7),
-        scratch=[pltpu.VMEM((1, rank), f32), pltpu.SMEM((sources,), jnp.int32), dma((6,)), dma((8,))],
+        scratch=[pltpu.VMEM((1, rank), f32), pltpu.SMEM((sources,), jnp.int32), dma((6,)), dma((1,))],
     )
     got = exchange(sent)
     sent, energy_owner = call(
-        functools.partial(owner_kernel, nz, width), [answer, scalar], [layers, got], flops=10**10,
+        functools.partial(owner_kernel, nz, width), [answer, scalar], [layers, got], flops=10**11,
     )
     got = exchange(sent)
     gradient, sent = call(
@@ -394,11 +395,13 @@
     )
     got = exchange(sent)
     (sent,) = call(
-        functools.partial(energy_kernel, nz, width), [struct((slabs, 8, LANES), f32)],
+        functools.partial(energy_kernel, nz, width), [struct((slabs, 1, LANES), f32)],
         [layers, got, energy_first, energy_owner, energy_next],
     )
     got = exchange(sent)
-    (gain,) = call(functools.partial(final_kernel, depth_count * columns), [struct((1, 1), f32)], [got])
+    gain, proposal = call(
+        functools.partial(final_kernel, depth_count * columns), [struct((1, 1), f32), field], [got, proposal]
+    )
     return (proposal, gain.reshape(1))
 
 

time: 62.1 us -> 61.3 us (0.987)
  Pallas kernels: 7.76 us -> 7.12 us
    pallas_call x6, Pallas kernels: 7.76 us -> 7.12 us  [call(): pl.pallas_call(kernel, out_shape=outs, in_specs=[far if i in hbm else vme...]
where the time goes in v6:
time: 61.3 us; the launch traced here: 61 us
  blocking collectives  53.2 us (87%)
  Pallas kernels  7.12 us (12%)
  between operations  0.65 us (1%)
    all_to_all x5, blocking collectives, exchange(): return lax.all_to_all(x, 'depth', 0, 0)  53.2 us
    pallas_call x6, Pallas kernels, call(): pl.pallas_call(kernel, out_shape=outs, in_specs=[far if i in hbm else vme...  7.12 us

profile of v6, /device:TPU:0, one launch (start us, length us, event | category | flops | bytes accessed | tf_op | source)
XLA Modules:
  0.0 61.0 jit_solution(15106361128944602971)
XLA Ops:
  0.6 1.8 %shard_map.95 = (f32[8,40,128]{2,1,0:T(8,128)S(1)}, f32[8,128]{1,0:T(8,128)S(1)}, s32[16,128]{1,0:T(8,128)S(1)}, f32[8,2048]{1,0:T(8,128)S(1)}, f32[1,2048]{1,0:...) custom-call(s32[16]{0:T(128)} %sd_hbm.1, ...), custom_call_target="tpu_custom_call" | custom-call | flops 1000000 | bytes 1000000 | tf_op jit(solution)/shard_map/pallas_call | solution.py:339
  2.5 14.7 %all_to_all.25.got_ref = f32[8,40,128]{2,1,0:T(8,128)S(1)} all-to-all(f32[8,40,128]{2,1,0:T(8,128)S(1)} %get-tuple-element.21), channel_id=1, replica_groups=mesh['chain'=4,'depth'=8] {'depth'}, dimensions={0} | all-to-all | bytes 327680 | tf_op jit(solution)/shard_map/all_to_all | solution.py:368
  17.1 0.0 copy-start
  17.1 0.2 shard_map.96
  17.3 10.4 %all_to_all.26.got_ref = f32[8,40,128]{2,1,0:T(8,128)S(1)} all-to-all(f32[8,40,128]{2,1,0:T(8,128)S(1)} %get-tuple-element.22), channel_id=1, replica_groups=mesh['chain'=4,'depth'=8] {'depth'}, dimensions={0} | all-to-all | bytes 327680 | tf_op jit(solution)/shard_map/all_to_all | solution.py:368
  27.7 0.0 copy-done
  27.7 2.7 %shard_map.97 = (f32[8,2048]{1,0:T(8,128)S(1)}, f32[8,16,128]{2,1,0:T(8,128)S(1)}) custom-call(s32[16,128]{1,0:T(8,128)S(1)} %get-tuple-element.20.layers_ref, f32[8,40,128]{2,1,0:T(8,128)S(1)} %all_to_all.26.got_ref, f32[8,2048]{1,0:T(8,128)S(1)} %get-tuple-element.23.model_ref, f32[1,2048]{1,0:T(1,128)S(1)} %get-tuple-element.24.rate_ref, ...), custom_call_target="tpu_custom_call" | custom-call | flops 1000000 | bytes 1000000 | tf_op jit(solution)/shard_map/pallas_call | solution.py:339
  30.4 9.3 %all_to_all.27.got_ref = f32[8,16,128]{2,1,0:T(8,128)S(1)} all-to-all(f32[8,16,128]{2,1,0:T(8,128)S(1)} %get-tuple-element.28), channel_id=1, replica_groups=mesh['chain'=4,'depth'=8] {'depth'}, dimensions={0} | all-to-all | bytes 131072 | tf_op jit(solution)/shard_map/all_to_all | solution.py:368
  39.7 1.7 %shard_map.98 = (f32[8,2048]{1,0:T(8,128)S(1)}, f32[8,40,128]{2,1,0:T(8,128)S(1)}, f32[8,128]{1,0:T(8,128)S(1)}) custom-call(s32[16,128]{1,0:T(8,128)S(1)} %get-tuple-element.20.layers_ref, f32[8,16,128]{2,1,0:T(8,128)S(1)} %all_to_all.27.got_ref, f32[16,128]{1,0:T(8,128)S(1)} %get-tuple-element.29.bends_ref, f32[8,2048]{1,0:T(8,128)S(1)} %get-tuple-element.30.gradient_ref, ...), custom_call_target="tpu_custom_call" | custom-call | flops 1000000 | bytes 1000000 | tf_op jit(solution)/shard_map/pallas_call | solution.py:339
  41.4 10.0 %all_to_all.28.got_ref = f32[8,40,128]{2,1,0:T(8,128)S(1)} all-to-all(f32[8,40,128]{2,1,0:T(8,128)S(1)} %get-tuple-element.31), channel_id=1, replica_groups=mesh['chain'=4,'depth'=8] {'depth'}, dimensions={0} | all-to-all | bytes 327680 | tf_op jit(solution)/shard_map/all_to_all | solution.py:368
  51.4 0.1 shard_map.99
  51.5 8.8 %all_to_all.29.got_ref = f32[8,1,128]{2,1,0:T(1,128)S(1)} all-to-all(f32[8,1,128]{2,1,0:T(1,128)S(1)} %shard_map.99), channel_id=1, replica_groups=mesh['chain'=4,'depth'=8] {'depth'}, dimensions={0} | all-to-all | bytes 8192 | tf_op jit(solution)/shard_map/all_to_all | solution.py:368
  60.3 0.6 %shard_map.100 = (f32[1,1]{1,0:T(1,128)}, f32[8,2048]{1,0:T(8,128)}) custom-call(f32[8,1,128]{2,1,0:T(1,128)S(1)} %all_to_all.29.got_ref, f32[8,2048]{1,0:T(8,128)S(1)} %get-tuple-element.35.proposal_in), custom_call_target="tpu_custom_call" | custom-call | flops 1000000 | bytes 1000000 | tf_op jit(solution)/shard_map/pallas_call | solution.py:339
Async XLA Ops:
  17.1 10.6 %copy-start = (bf16[256,8,2048]{2,1,0:T(8,128)(2,1)S(1)}, bf16[256,8,2048]{2,1,0:T(8,128)(2,1)}, u32[]{:S(2)}) copy-start(bf16[256,8,2048]{2,1,0:T(8,128)(2,1)} %param.13) | copy-start | bytes 25165828
